TPU v7x, 128 devices: a whole 4x4x4 slice. The times are simulated.
128 devices in a mesh: row: 8 (over z, core), col: 16 (over y, x).
Axes of the slice: x: 4, y: 4, z: 4, core: 2. Of those that a mesh axis runs over, the one named last changes fastest.
Arguments:
- load_amp: float32 [4096, 8192], P('row', 'col'), may hold values from 0.05 to 1
- load_mask: int32 [4096, 8192], P('row', 'col'), may hold values 0 or 1
- leak: float32 [4096, 8192], P('row', 'col'), may hold values from 0.001 to 0.05
- coarse_leak: float32 [1024, 2048], P('row', 'col'), may hold values from 0.01 to 0.5
- coarse_init: float32 [1024, 2048], P('row', 'col'), may hold values from 0 to 1
- via_fine: int32 [8, 32768], P('row', 'col'), may hold values from 0 to 262143
- via_coarse: int32 [8, 32768], P('row', 'col'), may hold values from 0 to 262143, as said below
- via_count: int32 [8, 256], P('row', 'col'), may hold values from 0 to 128, as said below
Outputs:
- fine_drop: float32 [4096, 8192], P('row', 'col')
- coarse_drop: float32 [1024, 2048], P('row', 'col')
Inputs may be any that keep to these rules, and one draw needn't show every extreme that they name: `via_coarse`: slot s of a tile names a coarse node whose stored column lies in s // 128 * 128 to s // 128 * 128 + 127. `via_count`: slots of an owner past its count are padding and carry arbitrary indices. In each tile row some owner gets 128 live slots from every tile of that row.
All inputs are finite; a program needn't handle non-finite values. No bound on the sum of `load_mask` on one device may be relied on, other than what follows from the above.
Results may differ from a plain program's by a relative error of at most 0.00022.
Values sent between devices are 32-bit elements; how exact they have to be, the bound alone decides.
A program may use at most 64 MiB of HBM per device.

v0:
```python
import functools

import jax
import jax.numpy as jnp
from jax import lax
from jax.sharding import Mesh
from jax.sharding import PartitionSpec as P

GROUP = 16
ITERS = 4
CSWEEP = 2
ROW_COL = ("row_0", "row_1", "col_0", "col_1")
ROW = ("row_0", "row_1")
COL = ("col_0", "col_1")


via_conductance = 2.0
coarse_conductance = 4.0
relaxation = 0.8


def padded_2(shard, sides, width):
    edges = {}
    for axis, dim in sides:
        size, length = (lax.axis_size(axis), shard.shape[dim])
        up = [(i, (i + 1) % size) for i in range(size - 1)]
        last = lax.slice_in_dim(shard, length - width, length, axis=dim)
        leading = lax.slice_in_dim(shard, 0, width, axis=dim)
        edges[dim] = (
            lax.ppermute(last, axis, up),
            lax.ppermute(leading, axis, [(b, a) for a, b in up]),
        )
    done = []
    for _, dim in sides:
        low, high = edges[dim]
        around = [(width, width) if d in done else (0, 0) for d in range(shard.ndim)]
        shard = jnp.concatenate([jnp.pad(low, around), shard, jnp.pad(high, around)], axis=dim)
        done.append(dim)
    return shard


def extended(block, sides, width, periodic):
    for axis, dim in sides:
        count = lax.axis_size(axis)
        forward = [(i, i + 1) for i in range(count - 1)]
        if periodic:
            forward.append((count - 1, 0))
        backward = [(target, source) for source, target in forward]
        low = lax.ppermute(
            lax.slice_in_dim(block, block.shape[dim] - width, None, axis=dim), axis, forward
        )
        high = lax.ppermute(lax.slice_in_dim(block, 0, width, axis=dim), axis, backward)
        block = jnp.concatenate([low, block, high], axis=dim)
    return block


def one_axis_at_a_time(shard, axes):
    return functools.reduce(lax.psum, axes, shard)


def fine_apply(field, diagonal):
    padded = padded_2(field, ((ROW, 0), (COL, 1)), 1)
    beside = padded[2:, 1:-1] + padded[:-2, 1:-1] + padded[1:-1, 2:] + padded[1:-1, :-2]
    return diagonal * field - beside


def coarse_apply(volt, diagonal):
    block_rows, block_cols = volt.shape
    groups = block_cols // GROUP
    stacked = extended(volt, ((ROW, 0),), 1, False)
    up_down = stacked[2:] + stacked[:-2]
    grouped = volt.reshape(block_rows, groups, GROUP)
    seam = jnp.stack([grouped[:, :, 0], grouped[:, :, GROUP - 1]], axis=0)
    edges = extended(seam, ((COL, 0),), 1, True)
    from_left = edges[0]
    from_right = edges[3]
    place = lax.axis_index(COL)
    width = lax.axis_size(COL)
    zero_col = jnp.zeros((block_rows, 1), jnp.float32)
    left_turned = jnp.concatenate([zero_col, from_left[:, :-1]], axis=1)
    from_left = jnp.where(place == 0, left_turned, from_left)
    right_turned = jnp.concatenate([from_right[:, 1:], zero_col], axis=1)
    from_right = jnp.where(place == width - 1, right_turned, from_right)
    left_full = jnp.concatenate([from_left[:, :, None], grouped[:, :, :-1]], axis=2).reshape(
        block_rows, block_cols
    )
    right_full = jnp.concatenate([grouped[:, :, 1:], from_right[:, :, None]], axis=2).reshape(
        block_rows, block_cols
    )
    return diagonal * volt - coarse_conductance * (up_down + left_full + right_full)


def paired_sum(first, second):
    return (
        one_axis_at_a_time(jnp.sum(first), ROW_COL),
        one_axis_at_a_time(jnp.sum(second), ROW_COL),
    )


def per_device(
    load_amp, load_mask, leak, coarse_leak, coarse_init, via_fine, via_coarse, via_count
):
    tile_rows, tile_cols = leak.shape
    block_rows, block_cols = coarse_leak.shape
    owners = lax.axis_size(COL)
    slot_count = via_fine.shape[1]
    per_owner = slot_count // owners
    row_width = block_cols * owners
    slot_all = jnp.arange(slot_count, dtype=jnp.int32)
    position = slot_all % per_owner
    live = position < jnp.repeat(via_count[0], per_owner)
    weight = jnp.where(live, via_conductance, 0.0).astype(jnp.float32)
    fine_index = via_fine[0]
    coarse_index = via_coarse[0]
    via_diag = jnp.zeros(tile_rows * tile_cols, jnp.float32).at[fine_index].add(weight)
    fine_diag = 4.0 + leak + via_diag.reshape(tile_rows, tile_cols)
    local_index = coarse_index // row_width * block_cols + coarse_index % row_width % block_cols
    request = jnp.where(live, local_index, -1).reshape(owners, per_owner)
    held = lax.all_to_all(request, COL, split_axis=0, concat_axis=0, tiled=True)
    held_valid = (held >= 0).reshape(-1)
    held_flat = jnp.where(held_valid, held.reshape(-1), 0)
    held_weight = jnp.where(held_valid, via_conductance, 0.0).astype(jnp.float32)
    coarse_count = (
        jnp.zeros(block_rows * block_cols, jnp.float32)
        .at[held_flat]
        .add(held_weight)
        .reshape(block_rows, block_cols)
    )
    coarse_diag = 4.0 * coarse_conductance + coarse_leak + coarse_count
    load = load_amp * load_mask.astype(jnp.float32)
    volt = coarse_init
    solution = jnp.zeros((tile_rows, tile_cols), jnp.float32)
    looked = jnp.where(held_valid, volt.reshape(-1)[held_flat], 0.0).reshape(owners, per_owner)
    at_via = lax.all_to_all(looked, COL, split_axis=0, concat_axis=0, tiled=True).reshape(-1)
    injected = jnp.zeros(tile_rows * tile_cols, jnp.float32).at[fine_index].add(weight * at_via)
    rhs = load + injected.reshape(tile_rows, tile_cols)
    residual = rhs - fine_apply(solution, fine_diag)
    precond = residual / fine_diag
    image = fine_apply(precond, fine_diag)
    product, curvature = paired_sum(residual * precond, image * precond)
    alpha = product / curvature
    direction = precond
    along = image
    for iteration in range(ITERS):
        solution = solution + alpha * direction
        residual = residual - alpha * along
        if iteration + 1 < ITERS:
            precond = residual / fine_diag
            image = fine_apply(precond, fine_diag)
            renewed, curvature = paired_sum(residual * precond, image * precond)
            ratio = renewed / product
            alpha = renewed / (curvature - ratio * renewed / alpha)
            direction = precond + ratio * direction
            along = image + ratio * along
            product = renewed
    at_fine = weight * solution.reshape(-1)[fine_index]
    arrived = lax.all_to_all(
        at_fine.reshape(owners, per_owner), COL, split_axis=0, concat_axis=0, tiled=True
    )
    sources = (
        jnp.zeros(block_rows * block_cols, jnp.float32)
        .at[held_flat]
        .add(arrived.reshape(-1))
        .reshape(block_rows, block_cols)
    )
    for sweep_turn in range(CSWEEP):
        volt = volt + relaxation * (sources - coarse_apply(volt, coarse_diag)) / coarse_diag
    return (solution, volt)


def solution(mesh):
    split = Mesh(mesh.devices.reshape(4, 2, 4, 4), ("row_0", "row_1", "col_0", "col_1"))
    in_specs = (
        P(ROW, COL),
        P(ROW, COL),
        P(ROW, COL),
        P(ROW, COL),
        P(ROW, COL),
        P(ROW, COL),
        P(ROW, COL),
        P(ROW, COL),
    )
    out_specs = (P(ROW, COL), P(ROW, COL))
    return jax.shard_map(
        per_device, mesh=split, in_specs=in_specs, out_specs=out_specs, check_vma=False
    )
```

profile of v0, /device:TPU:0, one launch (start us, length us, event | category | flops | bytes accessed | tf_op | source)
XLA Modules:
  0.0 358.9 jit_solution(15064754172412893006)
XLA Ops:
  2.0 4.6 %collective-permute-start.3 = (f32[512,1]{1,0:T(8,128)S(1)}, f32[512,1]{1,0:T(8,128)S(1)}, u32[]{:S(2)}, u32[]{:S(2)}) collective-permute-start(f32[512,1]{1,0:T(8,128)S(1)} %broadcast.399), channel_id=1, source_target_pairs={{0,1},{1,2},{2,3},{3,4},{4,5},{5,6},{6,7},{7,8},{8,9},{9,10},{10,1... | collective-permute-start | bytes 6152 | tf_op jit(solution)/shard_map/ppermute | solution.py:30
  7.8 3.0 collective-permute-start.1
  12.3 9.0 %all-to-all-start = ((s32[16,1,128]{2,1,0:T(1,128)}), s32[16,1,128]{2,1,0:T(1,128)S(1)}, u32[]{:S(2)}, u32[]{:S(2)}) async-start(s32[16,1,128]{2,1,0:T(1,128)} %compare_select_fusion.13), calls=%async_computation | async-start | bytes 16384 | tf_op jit(solution)/shard_map/all_to_all | solution.py:119
  22.8 5.2 %collective-permute-start.23 = (f32[1,128,8]{1,2,0:T(8,128)}, f32[1,128,8]{1,2,0:T(8,128)}, u32[]{:S(2)}, u32[]{:S(2)}) collective-permute-start(f32[1,128,8]{1,2,0:T(8,128)} %bitcast.20), channel_id=1, source_target_pairs={{1,0},{2,1},{3,2},{4,3},{5,4},{6,5},{7,6},{8,7},{9,8},{10,9},{11,1... | collective-permute-start | bytes 12296 | tf_op jit(solution)/shard_map/ppermute | solution.py:52
  28.8 11.8 %gather_fusion = f32[2048]{0:T(1024)S(1)} fusion(f32[16384]{0:T(1024)S(1)} %bitcast.77, s32[2048]{0:T(1024)S(1)} %broadcast_clamp_fusion.1), kind=kCustom, calls=%fused_computation | custom fusion | bytes 24576 | tf_op jit(solution)/shard_map/gather | solution.py:133
  41.3 3.5 all-to-all-start.1
  45.4 6.8 %all-to-all-done.1 = f32[16,1,128]{2,1,0:T(1,128)S(1)} async-done(((f32[16,1,128]{2,1,0:T(1,128)}), f32[16,1,128]{2,1,0:T(1,128)S(1)}, u32[]{:S(2)}, u32[]{:S(2)}) %all-to-all-start.1) | async-done | bytes 8224 | tf_op jit(solution)/shard_map/all_to_all | solution.py:134
  52.3 11.5 %scatter_custom_fusion = f32[262144]{0:T(1024)S(1)} fusion(s32[2048]{0:T(1024)S(1)} %bitcast.92, f32[2048]{0:T(1024)S(1)} %get-tuple-element.87, f32[]{:T(128)} %constant.72.clone.1), kind=kCustom, calls=%fused_computation.96 | custom fusion | flops 2048 | bytes 1048580 | tf_op jit(solution)/shard_map/scatter-add | solution.py:135
  63.9 11.5 %scatter_custom_fusion.1 = f32[262144]{0:T(1024)S(1)} fusion(s32[2048]{0:T(1024)S(1)} %bitcast.93, f32[2048]{0:T(1024)S(1)} %get-tuple-element.86, f32[]{:T(128)} %constant.72.clone.1), kind=kCustom, calls=%fused_computation.94 | custom fusion | flops 2048 | bytes 1048580 | tf_op jit(solution)/shard_map/scatter-add | solution.py:115
  78.0 3.1 fusion.75
  82.6 4.6 %collective-permute-start.7 = (f32[512,1]{1,0:T(8,128)S(1)}, f32[512,1]{1,0:T(8,128)S(1)}, u32[]{:S(2)}, u32[]{:S(2)}) collective-permute-start(f32[512,1]{1,0:T(8,128)S(1)} %get-tuple-element.69), channel_id=1, source_target_pairs={{0,1},{1,2},{2,3},{3,4},{4,5},{5,6},{6,7},{7,8},{8,9},{9,10},{10,1... | collective-permute-start | bytes 6152 | tf_op jit(solution)/shard_map/ppermute | solution.py:30
  88.4 3.0 collective-permute-start.5
  93.7 14.1 %all-reduce.27 = (f32[]{:T(128)}, f32[]{:T(128)}) all-reduce(f32[]{:T(128)} %get-tuple-element.11, f32[]{:T(128)} %get-tuple-element.10), channel_id=1, replica_groups=mesh['row_0'=4,'row_1'=2,'col_0'=4,'col_1'=4] {'row_0'}, use_global_device_ids=true, to_apply=%region_3.4 | all-reduce | flops 2 | bytes 16 | tf_op jit(solution)/shard_map/psum | solution.py:58
  107.8 3.1 all-reduce.31
  110.9 10.6 %all-reduce.23 = (f32[]{:T(128)}, f32[]{:T(128)}) all-reduce(f32[]{:T(128)} %get-tuple-element.42, f32[]{:T(128)} %get-tuple-element.43), channel_id=1, replica_groups=mesh['row_0'=4,'row_1'=2,'col_0'=4,'col_1'=4] {'col_0'}, use_global_device_ids=true, to_apply=%region_5.6 | all-reduce | flops 2 | bytes 16 | tf_op jit(solution)/shard_map/psum | solution.py:58
  121.5 10.0 %all-reduce.19 = (f32[]{:T(128)}, f32[]{:T(128)}) all-reduce(f32[]{:T(128)} %get-tuple-element.26, f32[]{:T(128)} %get-tuple-element.27), channel_id=1, replica_groups=mesh['row_0'=4,'row_1'=2,'col_0'=4,'col_1'=4] {'col_1'}, use_global_device_ids=true, to_apply=%region_6.7 | all-reduce | flops 2 | bytes 16 | tf_op jit(solution)/shard_map/psum | solution.py:58
  132.8 2.6 fusion.73
  138.4 5.3 %collective-permute-start.11 = (f32[512,1]{1,0:T(8,128)}, f32[512,1]{1,0:T(8,128)}, u32[]{:S(2)}, u32[]{:S(2)}) collective-permute-start(f32[512,1]{1,0:T(8,128)} %get-tuple-element.65), channel_id=1, source_target_pairs={{0,1},{1,2},{2,3},{3,4},{4,5},{5,6},{6,7},{7,8},{8,9},{9,10},{10,1... | collective-permute-start | bytes 6152 | tf_op jit(solution)/shard_map/ppermute | solution.py:30
  144.9 3.6 %collective-permute-start.9 = (f32[1,512]{1,0:T(1,128)}, f32[1,512]{1,0:T(1,128)}, u32[]{:S(2)}, u32[]{:S(2)}) collective-permute-start(f32[1,512]{1,0:T(1,128)} %get-tuple-element.66), channel_id=1, source_target_pairs={{0,16},{16,32},{32,48},{48,64},{64,80},{80,96},{96,112},{1,17},{17... | collective-permute-start | bytes 6152 | tf_op jit(solution)/shard_map/ppermute | solution.py:30
  149.8 5.7 %multiply_reduce_fusion.3 = (f32[]{:T(128)}, f32[]{:T(128)}, f32[512,512]{1,0:T(8,128)}) fusion(f32[512,512]{1,0:T(8,128)} %copy-done.2, f32[512,512]{1,0:T(8,128)} %get-tuple-element.51, f32[1,512]{1,0:T(1,128)} %collective-permute-done.8, f32[1,512]{1,0:T(1,128)} %collective-permute-done.9, f32[512,1]{1,0:T(8,128)} %collective-permute-done.11, ...), kind=kLoop, calls=%fused_computation.88 | loop fusion | flops 6029310 | bytes 4202504 | tf_op jit(solution)/shard_map/reduce_sum | solution.py:96
  155.5 9.7 %all-reduce.26 = (f32[]{:T(128)}, f32[]{:T(128)}) all-reduce(f32[]{:T(128)} %get-tuple-element.9, f32[]{:T(128)} %get-tuple-element.8), channel_id=1, replica_groups=mesh['row_0'=4,'row_1'=2,'col_0'=4,'col_1'=4] {'row_0'}, use_global_device_ids=true, to_apply=%region_13.14 | all-reduce | flops 2 | bytes 16 | tf_op jit(solution)/shard_map/psum | solution.py:58
  165.2 3.1 all-reduce.30
  168.3 9.1 %all-reduce.22 = (f32[]{:T(128)}, f32[]{:T(128)}) all-reduce(f32[]{:T(128)} %get-tuple-element.40, f32[]{:T(128)} %get-tuple-element.41), channel_id=1, replica_groups=mesh['row_0'=4,'row_1'=2,'col_0'=4,'col_1'=4] {'col_0'}, use_global_device_ids=true, to_apply=%region_15.16 | all-reduce | flops 2 | bytes 16 | tf_op jit(solution)/shard_map/psum | solution.py:58
  177.4 12.3 %all-reduce.18 = (f32[]{:T(128)}, f32[]{:T(128)}) all-reduce(f32[]{:T(128)} %get-tuple-element.24, f32[]{:T(128)} %get-tuple-element.25), channel_id=1, replica_groups=mesh['row_0'=4,'row_1'=2,'col_0'=4,'col_1'=4] {'col_1'}, use_global_device_ids=true, to_apply=%region_16.17 | all-reduce | flops 2 | bytes 16 | tf_op jit(solution)/shard_map/psum | solution.py:58
  193.8 2.0 fusion.71
  197.3 4.6 %collective-permute-start.15 = (f32[512,1]{1,0:T(8,128)S(1)}, f32[512,1]{1,0:T(8,128)S(1)}, u32[]{:S(2)}, u32[]{:S(2)}) collective-permute-start(f32[512,1]{1,0:T(8,128)S(1)} %get-tuple-element.61), channel_id=1, source_target_pairs={{0,1},{1,2},{2,3},{3,4},{4,5},{5,6},{6,7},{7,8},{8,9},{9,10},{10,1... | collective-permute-start | bytes 6152 | tf_op jit(solution)/shard_map/ppermute | solution.py:30
  203.2 3.0 collective-permute-start.13
  207.0 1.5 collective-permute-start.20
  208.5 2.3 multiply_reduce_fusion.1
  210.8 12.2 %all-reduce.25 = (f32[]{:T(128)}, f32[]{:T(128)}) all-reduce(f32[]{:T(128)} %get-tuple-element.7, f32[]{:T(128)} %get-tuple-element.6), channel_id=1, replica_groups=mesh['row_0'=4,'row_1'=2,'col_0'=4,'col_1'=4] {'row_0'}, use_global_device_ids=true, to_apply=%region_23.24 | all-reduce | flops 2 | bytes 16 | tf_op jit(solution)/shard_map/psum | solution.py:58
  223.0 3.1 all-reduce.29
  226.1 8.4 %all-reduce.21 = (f32[]{:T(128)}, f32[]{:T(128)}) all-reduce(f32[]{:T(128)} %get-tuple-element.38, f32[]{:T(128)} %get-tuple-element.39), channel_id=1, replica_groups=mesh['row_0'=4,'row_1'=2,'col_0'=4,'col_1'=4] {'col_0'}, use_global_device_ids=true, to_apply=%region_25.26 | all-reduce | flops 2 | bytes 16 | tf_op jit(solution)/shard_map/psum | solution.py:58
  234.5 10.2 %all-reduce.17 = (f32[]{:T(128)}, f32[]{:T(128)}) all-reduce(f32[]{:T(128)} %get-tuple-element.22, f32[]{:T(128)} %get-tuple-element.23), channel_id=1, replica_groups=mesh['row_0'=4,'row_1'=2,'col_0'=4,'col_1'=4] {'col_1'}, use_global_device_ids=true, to_apply=%region_26.27 | all-reduce | flops 2 | bytes 16 | tf_op jit(solution)/shard_map/psum | solution.py:58
  248.3 2.5 fusion.69
  252.3 4.6 %collective-permute-start.19 = (f32[512,1]{1,0:T(8,128)S(1)}, f32[512,1]{1,0:T(8,128)S(1)}, u32[]{:S(2)}, u32[]{:S(2)}) collective-permute-start(f32[512,1]{1,0:T(8,128)S(1)} %get-tuple-element.57), channel_id=1, source_target_pairs={{0,1},{1,2},{2,3},{3,4},{4,5},{5,6},{6,7},{7,8},{8,9},{9,10},{10,1... | collective-permute-start | bytes 6152 | tf_op jit(solution)/shard_map/ppermute | solution.py:30
  258.2 3.0 collective-permute-start.17
  261.3 1.9 collective-permute-start.21
  264.7 9.3 %all-reduce.24 = (f32[]{:T(128)}, f32[]{:T(128)}) all-reduce(f32[]{:T(128)} %get-tuple-element.5, f32[]{:T(128)} %get-tuple-element.4), channel_id=1, replica_groups=mesh['row_0'=4,'row_1'=2,'col_0'=4,'col_1'=4] {'row_0'}, use_global_device_ids=true, to_apply=%region_33.34 | all-reduce | flops 2 | bytes 16 | tf_op jit(solution)/shard_map/psum | solution.py:58
  274.0 3.1 all-reduce.28
  277.1 10.4 %all-reduce.20 = (f32[]{:T(128)}, f32[]{:T(128)}) all-reduce(f32[]{:T(128)} %get-tuple-element.36, f32[]{:T(128)} %get-tuple-element.37), channel_id=1, replica_groups=mesh['row_0'=4,'row_1'=2,'col_0'=4,'col_1'=4] {'col_0'}, use_global_device_ids=true, to_apply=%region_35.36 | all-reduce | flops 2 | bytes 16 | tf_op jit(solution)/shard_map/psum | solution.py:58
  287.5 10.7 %all-reduce.16 = (f32[]{:T(128)}, f32[]{:T(128)}) all-reduce(f32[]{:T(128)} %get-tuple-element.20, f32[]{:T(128)} %get-tuple-element.21), channel_id=1, replica_groups=mesh['row_0'=4,'row_1'=2,'col_0'=4,'col_1'=4] {'col_1'}, use_global_device_ids=true, to_apply=%region_36.37 | all-reduce | flops 2 | bytes 16 | tf_op jit(solution)/shard_map/psum | solution.py:58
  301.8 2.1 multiply_add_fusion
  304.8 11.8 %gather_fusion.1 = f32[2048]{0:T(1024)S(1)} fusion(f32[262144]{0:T(1024)S(1)} %bitcast.78, s32[2048]{0:T(1024)S(1)} %copy-done.12), kind=kCustom, calls=%fused_computation.1 | custom fusion | bytes 24576 | tf_op jit(solution)/shard_map/gather | solution.py:156
  317.3 3.4 all-to-all-start.2
  321.0 13.3 %scatter_custom_fusion.3 = f32[16384]{0:T(1024)S(1)} fusion(s32[2048]{0:T(1024)S(1)} %bitcast.90, f32[2048]{0:T(1024)} %bitcast.105, f32[]{:T(128)} %constant.72.clone.1), kind=kCustom, calls=%fused_computation.132 | custom fusion | flops 2048 | bytes 66048 | tf_op jit(solution)/shard_map/scatter-add | solution.py:126
  334.3 13.1 %scatter_custom_fusion.2 = f32[16384]{0:T(1024)S(1)} fusion(s32[2048]{0:T(1024)S(1)} %bitcast.91, f32[2048]{0:T(1024)S(1)} %bitcast.104, f32[]{:T(128)} %constant.72.clone.1), kind=kCustom, calls=%fused_computation.134 | custom fusion | flops 2048 | bytes 65540 | tf_op jit(solution)/shard_map/scatter-add | solution.py:163
  347.8 5.3 %collective-permute-start.27 = (f32[1,128,8]{1,2,0:T(8,128)S(1)}, f32[1,128,8]{1,2,0:T(8,128)S(1)}, u32[]{:S(2)}, u32[]{:S(2)}) collective-permute-start(f32[1,128,8]{1,2,0:T(8,128)S(1)} %bitcast.110), channel_id=1, source_target_pairs={{1,0},{2,1},{3,2},{4,3},{5,4},{6,5},{7,6},{8,7},{9,8},{10,9},{11,1... | collective-permute-start | bytes 12296 | tf_op jit(solution)/shard_map/ppermute | solution.py:52
  354.3 3.0 collective-permute-start.25
  (128 shorter events, 33.2 us)
Async XLA Ops:
  0.6 28.2 %copy-start = (f32[128,128]{1,0:T(8,128)S(1)}, f32[128,128]{1,0:T(8,128)}, u32[]{:S(2)}) copy-start(f32[128,128]{1,0:T(8,128)} %param.12) | copy-start | bytes 196612
  0.7 75.9 %collective-permute-start.2 = (f32[512,1]{1,0:T(8,128)S(1)}, f32[512,1]{1,0:T(8,128)S(1)}, u32[]{:S(2)}, u32[]{:S(2)}) collective-permute-start(f32[512,1]{1,0:T(8,128)S(1)} %broadcast.399), channel_id=1, source_target_pairs={{1,0},{2,1},{3,2},{4,3},{5,4},{6,5},{7,6},{8,7},{9,8},{10,9},{11,1... | collective-permute-start | bytes 6152 | tf_op jit(solution)/shard_map/ppermute | solution.py:31
  2.0 74.6 %collective-permute-start.3 = (f32[512,1]{1,0:T(8,128)S(1)}, f32[512,1]{1,0:T(8,128)S(1)}, u32[]{:S(2)}, u32[]{:S(2)}) collective-permute-start(f32[512,1]{1,0:T(8,128)S(1)} %broadcast.399), channel_id=1, source_target_pairs={{0,1},{1,2},{2,3},{3,4},{4,5},{5,6},{6,7},{7,8},{8,9},{9,10},{10,1... | collective-permute-start | bytes 6152 | tf_op jit(solution)/shard_map/ppermute | solution.py:30
  6.5 70.1 %collective-permute-start = (f32[1,512]{1,0:T(1,128)S(1)}, f32[1,512]{1,0:T(1,128)S(1)}, u32[]{:S(2)}, u32[]{:S(2)}) collective-permute-start(f32[1,512]{1,0:T(1,128)S(1)} %broadcast.398), channel_id=1, source_target_pairs={{16,0},{32,16},{48,32},{64,48},{80,64},{96,80},{112,96},{17,1},{33... | collective-permute-start | bytes 6152 | tf_op jit(solution)/shard_map/ppermute | solution.py:31
  7.8 68.8 %collective-permute-start.1 = (f32[1,512]{1,0:T(1,128)S(1)}, f32[1,512]{1,0:T(1,128)S(1)}, u32[]{:S(2)}, u32[]{:S(2)}) collective-permute-start(f32[1,512]{1,0:T(1,128)S(1)} %broadcast.398), channel_id=1, source_target_pairs={{0,16},{16,32},{32,48},{48,64},{64,80},{80,96},{96,112},{1,17},{17... | collective-permute-start | bytes 6152 | tf_op jit(solution)/shard_map/ppermute | solution.py:30
  12.3 16.5 %all-to-all-start = ((s32[16,1,128]{2,1,0:T(1,128)}), s32[16,1,128]{2,1,0:T(1,128)S(1)}, u32[]{:S(2)}, u32[]{:S(2)}) async-start(s32[16,1,128]{2,1,0:T(1,128)} %compare_select_fusion.13), calls=%async_computation | async-start | bytes 16384 | tf_op jit(solution)/shard_map/all_to_all | solution.py:119
  22.8 126.3 %collective-permute-start.23 = (f32[1,128,8]{1,2,0:T(8,128)}, f32[1,128,8]{1,2,0:T(8,128)}, u32[]{:S(2)}, u32[]{:S(2)}) collective-permute-start(f32[1,128,8]{1,2,0:T(8,128)} %bitcast.20), channel_id=1, source_target_pairs={{1,0},{2,1},{3,2},{4,3},{5,4},{6,5},{7,6},{8,7},{9,8},{10,9},{11,1... | collective-permute-start | bytes 12296 | tf_op jit(solution)/shard_map/ppermute | solution.py:52
  28.8 23.4 %copy-start.13 = (s32[1,16]{1,0:T(1,128)S(1)}, s32[1,16]{1,0:T(1,128)}, u32[]{:S(2)}) copy-start(s32[1,16]{1,0:T(1,128)} %param.15) | copy-start | bytes 196
  41.3 10.9 %all-to-all-start.1 = ((f32[16,1,128]{2,1,0:T(1,128)}), f32[16,1,128]{2,1,0:T(1,128)S(1)}, u32[]{:S(2)}, u32[]{:S(2)}) async-start(f32[16,1,128]{2,1,0:T(1,128)} %get-tuple-element.85), calls=%async_computation.1 | async-start | bytes 16384 | tf_op jit(solution)/shard_map/all_to_all | solution.py:134
  76.6 1.4 copy-start.7
  76.6 0.7 copy-start.9
  81.1 12.6 %copy-start.5 = (f32[512,512]{1,0:T(8,128)}, f32[512,512]{1,0:T(8,128)S(1)}, u32[]{:S(2)}) copy-start(f32[512,512]{1,0:T(8,128)S(1)} %get-tuple-element.54) | copy-start | bytes 3145732
  81.3 10.8 %collective-permute-start.6 = (f32[512,1]{1,0:T(8,128)S(1)}, f32[512,1]{1,0:T(8,128)S(1)}, u32[]{:S(2)}, u32[]{:S(2)}) collective-permute-start(f32[512,1]{1,0:T(8,128)S(1)} %get-tuple-element.68), channel_id=1, source_target_pairs={{1,0},{2,1},{3,2},{4,3},{5,4},{6,5},{7,6},{8,7},{9,8},{10,9},{11,1... | collective-permute-start | bytes 6152 | tf_op jit(solution)/shard_map/ppermute | solution.py:31
  82.6 9.5 %collective-permute-start.7 = (f32[512,1]{1,0:T(8,128)S(1)}, f32[512,1]{1,0:T(8,128)S(1)}, u32[]{:S(2)}, u32[]{:S(2)}) collective-permute-start(f32[512,1]{1,0:T(8,128)S(1)} %get-tuple-element.69), channel_id=1, source_target_pairs={{0,1},{1,2},{2,3},{3,4},{4,5},{5,6},{6,7},{7,8},{8,9},{9,10},{10,1... | collective-permute-start | bytes 6152 | tf_op jit(solution)/shard_map/ppermute | solution.py:30
  87.1 5.0 %collective-permute-start.4 = (f32[1,512]{1,0:T(1,128)S(1)}, f32[1,512]{1,0:T(1,128)S(1)}, u32[]{:S(2)}, u32[]{:S(2)}) collective-permute-start(f32[1,512]{1,0:T(1,128)S(1)} %get-tuple-element.71), channel_id=1, source_target_pairs={{16,0},{32,16},{48,32},{64,48},{80,64},{96,80},{112,96},{17,1},{33... | collective-permute-start | bytes 6152 | tf_op jit(solution)/shard_map/ppermute | solution.py:31
  88.4 3.8 %collective-permute-start.5 = (f32[1,512]{1,0:T(1,128)S(1)}, f32[1,512]{1,0:T(1,128)S(1)}, u32[]{:S(2)}, u32[]{:S(2)}) collective-permute-start(f32[1,512]{1,0:T(1,128)S(1)} %get-tuple-element.70), channel_id=1, source_target_pairs={{0,16},{16,32},{32,48},{48,64},{64,80},{80,96},{96,112},{1,17},{17... | collective-permute-start | bytes 6152 | tf_op jit(solution)/shard_map/ppermute | solution.py:30
  135.4 1.1 copy-start.2
  137.1 12.7 %collective-permute-start.10 = (f32[512,1]{1,0:T(8,128)}, f32[512,1]{1,0:T(8,128)S(1)}, u32[]{:S(2)}, u32[]{:S(2)}) collective-permute-start(f32[512,1]{1,0:T(8,128)} %get-tuple-element.64), channel_id=1, source_target_pairs={{1,0},{2,1},{3,2},{4,3},{5,4},{6,5},{7,6},{8,7},{9,8},{10,9},{11,1... | collective-permute-start | bytes 6152 | tf_op jit(solution)/shard_map/ppermute | solution.py:31
  138.4 11.4 %collective-permute-start.11 = (f32[512,1]{1,0:T(8,128)}, f32[512,1]{1,0:T(8,128)}, u32[]{:S(2)}, u32[]{:S(2)}) collective-permute-start(f32[512,1]{1,0:T(8,128)} %get-tuple-element.65), channel_id=1, source_target_pairs={{0,1},{1,2},{2,3},{3,4},{4,5},{5,6},{6,7},{7,8},{8,9},{9,10},{10,1... | collective-permute-start | bytes 6152 | tf_op jit(solution)/shard_map/ppermute | solution.py:30
  143.6 6.2 %collective-permute-start.8 = (f32[1,512]{1,0:T(1,128)}, f32[1,512]{1,0:T(1,128)}, u32[]{:S(2)}, u32[]{:S(2)}) collective-permute-start(f32[1,512]{1,0:T(1,128)} %get-tuple-element.67), channel_id=1, source_target_pairs={{16,0},{32,16},{48,32},{64,48},{80,64},{96,80},{112,96},{17,1},{33... | collective-permute-start | bytes 6152 | tf_op jit(solution)/shard_map/ppermute | solution.py:31
  144.9 4.9 %collective-permute-start.9 = (f32[1,512]{1,0:T(1,128)}, f32[1,512]{1,0:T(1,128)}, u32[]{:S(2)}, u32[]{:S(2)}) collective-permute-start(f32[1,512]{1,0:T(1,128)} %get-tuple-element.66), channel_id=1, source_target_pairs={{0,16},{16,32},{32,48},{48,64},{64,80},{80,96},{96,112},{1,17},{17... | collective-permute-start | bytes 6152 | tf_op jit(solution)/shard_map/ppermute | solution.py:30
  149.1 109.1 %collective-permute-start.22 = (f32[1,128,8]{1,2,0:T(8,128)}, f32[1,128,8]{1,2,0:T(8,128)S(1)}, u32[]{:S(2)}, u32[]{:S(2)}) collective-permute-start(f32[1,128,8]{1,2,0:T(8,128)} %bitcast.16), channel_id=1, source_target_pairs={{0,1},{1,2},{2,3},{3,4},{4,5},{5,6},{6,7},{7,8},{8,9},{9,10},{10,1... | collective-permute-start | bytes 12296 | tf_op jit(solution)/shard_map/ppermute | solution.py:49
  195.9 14.9 %copy-start.4 = (f32[512,512]{1,0:T(8,128)}, f32[512,512]{1,0:T(8,128)S(1)}, u32[]{:S(2)}) copy-start(f32[512,512]{1,0:T(8,128)S(1)} %get-tuple-element.47) | copy-start | bytes 3145732
  195.9 14.9 %copy-start.6 = (f32[512,512]{1,0:T(8,128)}, f32[512,512]{1,0:T(8,128)S(1)}, u32[]{:S(2)}) copy-start(f32[512,512]{1,0:T(8,128)S(1)} %get-tuple-element.48) | copy-start | bytes 3145732
  195.9 11.1 %copy-start.18 = (f32[1,128]{1,0:T(1,128)S(1)}, f32[1,128]{1,0:T(1,128)}, u32[]{:S(2)}) copy-start(f32[1,128]{1,0:T(1,128)} %get-tuple-element.78) | copy-start | bytes 1540
  196.0 10.9 %collective-permute-start.14 = (f32[512,1]{1,0:T(8,128)S(1)}, f32[512,1]{1,0:T(8,128)S(1)}, u32[]{:S(2)}, u32[]{:S(2)}) collective-permute-start(f32[512,1]{1,0:T(8,128)S(1)} %get-tuple-element.60), channel_id=1, source_target_pairs={{1,0},{2,1},{3,2},{4,3},{5,4},{6,5},{7,6},{8,7},{9,8},{10,9},{11,1... | collective-permute-start | bytes 6152 | tf_op jit(solution)/shard_map/ppermute | solution.py:31
  197.3 11.1 %collective-permute-start.15 = (f32[512,1]{1,0:T(8,128)S(1)}, f32[512,1]{1,0:T(8,128)S(1)}, u32[]{:S(2)}, u32[]{:S(2)}) collective-permute-start(f32[512,1]{1,0:T(8,128)S(1)} %get-tuple-element.61), channel_id=1, source_target_pairs={{0,1},{1,2},{2,3},{3,4},{4,5},{5,6},{6,7},{7,8},{8,9},{9,10},{10,1... | collective-permute-start | bytes 6152 | tf_op jit(solution)/shard_map/ppermute | solution.py:30
  201.9 6.5 %collective-permute-start.12 = (f32[1,512]{1,0:T(1,128)S(1)}, f32[1,512]{1,0:T(1,128)S(1)}, u32[]{:S(2)}, u32[]{:S(2)}) collective-permute-start(f32[1,512]{1,0:T(1,128)S(1)} %get-tuple-element.63), channel_id=1, source_target_pairs={{16,0},{32,16},{48,32},{64,48},{80,64},{96,80},{112,96},{17,1},{33... | collective-permute-start | bytes 6152 | tf_op jit(solution)/shard_map/ppermute | solution.py:31
  203.2 5.2 %collective-permute-start.13 = (f32[1,512]{1,0:T(1,128)S(1)}, f32[1,512]{1,0:T(1,128)S(1)}, u32[]{:S(2)}, u32[]{:S(2)}) collective-permute-start(f32[1,512]{1,0:T(1,128)S(1)} %get-tuple-element.62), channel_id=1, source_target_pairs={{0,16},{16,32},{32,48},{48,64},{64,80},{80,96},{96,112},{1,17},{17... | collective-permute-start | bytes 6152 | tf_op jit(solution)/shard_map/ppermute | solution.py:30
  207.0 140.5 %collective-permute-start.20 = (f32[1,128]{1,0:T(1,128)S(1)}, f32[1,128]{1,0:T(1,128)S(1)}, u32[]{:S(2)}, u32[]{:S(2)}) collective-permute-start(f32[1,128]{1,0:T(1,128)S(1)} %copy-done.18), channel_id=1, source_target_pairs={{16,0},{32,16},{48,32},{64,48},{80,64},{96,80},{112,96},{17,1},{33... | collective-permute-start | bytes 1544 | tf_op jit(solution)/shard_map/ppermute | solution.py:52
  250.8 13.8 %copy-start.1 = (f32[512,512]{1,0:T(8,128)}, f32[512,512]{1,0:T(8,128)S(1)}, u32[]{:S(2)}) copy-start(f32[512,512]{1,0:T(8,128)S(1)} %get-tuple-element.44) | copy-start | bytes 3145732
  250.9 10.4 %copy-start.17 = (f32[1,128]{1,0:T(1,128)S(1)}, f32[1,128]{1,0:T(1,128)}, u32[]{:S(2)}) copy-start(f32[1,128]{1,0:T(1,128)} %get-tuple-element.79) | copy-start | bytes 1540
  251.0 10.2 %collective-permute-start.18 = (f32[512,1]{1,0:T(8,128)S(1)}, f32[512,1]{1,0:T(8,128)S(1)}, u32[]{:S(2)}, u32[]{:S(2)}) collective-permute-start(f32[512,1]{1,0:T(8,128)S(1)} %get-tuple-element.56), channel_id=1, source_target_pairs={{1,0},{2,1},{3,2},{4,3},{5,4},{6,5},{7,6},{8,7},{9,8},{10,9},{11,1... | collective-permute-start | bytes 6152 | tf_op jit(solution)/shard_map/ppermute | solution.py:31
  252.3 10.9 %collective-permute-start.19 = (f32[512,1]{1,0:T(8,128)S(1)}, f32[512,1]{1,0:T(8,128)S(1)}, u32[]{:S(2)}, u32[]{:S(2)}) collective-permute-start(f32[512,1]{1,0:T(8,128)S(1)} %get-tuple-element.57), channel_id=1, source_target_pairs={{0,1},{1,2},{2,3},{3,4},{4,5},{5,6},{6,7},{7,8},{8,9},{9,10},{10,1... | collective-permute-start | bytes 6152 | tf_op jit(solution)/shard_map/ppermute | solution.py:30
  256.9 6.3 %collective-permute-start.16 = (f32[1,512]{1,0:T(1,128)S(1)}, f32[1,512]{1,0:T(1,128)S(1)}, u32[]{:S(2)}, u32[]{:S(2)}) collective-permute-start(f32[1,512]{1,0:T(1,128)S(1)} %get-tuple-element.59), channel_id=1, source_target_pairs={{16,0},{32,16},{48,32},{64,48},{80,64},{96,80},{112,96},{17,1},{33... | collective-permute-start | bytes 6152 | tf_op jit(solution)/shard_map/ppermute | solution.py:31
  258.2 5.0 %collective-permute-start.17 = (f32[1,512]{1,0:T(1,128)S(1)}, f32[1,512]{1,0:T(1,128)S(1)}, u32[]{:S(2)}, u32[]{:S(2)}) collective-permute-start(f32[1,512]{1,0:T(1,128)S(1)} %get-tuple-element.58), channel_id=1, source_target_pairs={{0,16},{16,32},{32,48},{48,64},{64,80},{80,96},{96,112},{1,17},{17... | collective-permute-start | bytes 6152 | tf_op jit(solution)/shard_map/ppermute | solution.py:30
  261.3 86.1 %collective-permute-start.21 = (f32[1,128]{1,0:T(1,128)S(1)}, f32[1,128]{1,0:T(1,128)S(1)}, u32[]{:S(2)}, u32[]{:S(2)}) collective-permute-start(f32[1,128]{1,0:T(1,128)S(1)} %copy-done.17), channel_id=1, source_target_pairs={{0,16},{16,32},{32,48},{48,64},{64,80},{80,96},{96,112},{1,17},{17... | collective-permute-start | bytes 1544 | tf_op jit(solution)/shard_map/ppermute | solution.py:49
  263.2 38.5 %copy-start.3 = (f32[512,512]{1,0:T(8,128)S(1)}, f32[512,512]{1,0:T(8,128)}, u32[]{:S(2)}) copy-start(f32[512,512]{1,0:T(8,128)} %copy-done.2) | copy-start | bytes 3145732
  303.9 1.0 copy-start.8
  303.9 1.0 copy-start.12
  304.8 11.8 %copy-start.14 = (s32[1,16]{1,0:T(1,128)S(1)}, s32[1,16]{1,0:T(1,128)}, u32[]{:S(2)}) copy-start(s32[1,16]{1,0:T(1,128)} %param.15) | copy-start | bytes 196
  304.8 15.9 %copy-start.11 = (f32[128,8,15]{0,2,1:T(8,128)S(1)}, f32[128,8,15]{0,2,1:T(8,128)}, u32[]{:S(2)}) copy-start(f32[128,8,15]{0,2,1:T(8,128)} %get-tuple-element.83) | copy-start | bytes 184324
  304.8 42.6 %copy-start.10 = (f32[128,128]{1,0:T(8,128)S(1)}, f32[128,128]{1,0:T(8,128)}, u32[]{:S(2)}) copy-start(f32[128,128]{1,0:T(8,128)} %param.11) | copy-start | bytes 196612
  317.3 17.0 %all-to-all-start.2 = ((f32[16,1,128]{2,1,0:T(1,128)}), f32[16,1,128]{2,1,0:T(1,128)S(1)}, u32[]{:S(2)}, u32[]{:S(2)}) async-start(f32[16,1,128]{2,1,0:T(1,128)} %fusion.61), calls=%async_computation.2 | async-start | bytes 16384 | tf_op jit(solution)/shard_map/all_to_all | solution.py:157
  347.6 9.8 %collective-permute-start.26 = (f32[1,128,8]{1,2,0:T(8,128)S(1)}, f32[1,128,8]{1,2,0:T(8,128)S(1)}, u32[]{:S(2)}, u32[]{:S(2)}) collective-permute-start(f32[1,128,8]{1,2,0:T(8,128)S(1)} %bitcast.109), channel_id=1, source_target_pairs={{0,1},{1,2},{2,3},{3,4},{4,5},{5,6},{6,7},{7,8},{8,9},{9,10},{10,1... | collective-permute-start | bytes 12296 | tf_op jit(solution)/shard_map/ppermute | solution.py:49
  347.8 9.6 %collective-permute-start.27 = (f32[1,128,8]{1,2,0:T(8,128)S(1)}, f32[1,128,8]{1,2,0:T(8,128)S(1)}, u32[]{:S(2)}, u32[]{:S(2)}) collective-permute-start(f32[1,128,8]{1,2,0:T(8,128)S(1)} %bitcast.110), channel_id=1, source_target_pairs={{1,0},{2,1},{3,2},{4,3},{5,4},{6,5},{7,6},{8,7},{9,8},{10,9},{11,1... | collective-permute-start | bytes 12296 | tf_op jit(solution)/shard_map/ppermute | solution.py:52
  353.0 4.6 %collective-permute-start.24 = (f32[1,128]{1,0:T(1,128)S(1)}, f32[1,128]{1,0:T(1,128)S(1)}, u32[]{:S(2)}, u32[]{:S(2)}) collective-permute-start(f32[1,128]{1,0:T(1,128)S(1)} %get-tuple-element.72), channel_id=1, source_target_pairs={{16,0},{32,16},{48,32},{64,48},{80,64},{96,80},{112,96},{17,1},{33... | collective-permute-start | bytes 1544 | tf_op jit(solution)/shard_map/ppermute | solution.py:52
  354.3 3.8 %collective-permute-start.25 = (f32[1,128]{1,0:T(1,128)S(1)}, f32[1,128]{1,0:T(1,128)S(1)}, u32[]{:S(2)}, u32[]{:S(2)}) collective-permute-start(f32[1,128]{1,0:T(1,128)S(1)} %get-tuple-element.73), channel_id=1, source_target_pairs={{0,16},{16,32},{32,48},{48,64},{64,80},{80,96},{96,112},{1,17},{17... | collective-permute-start | bytes 1544 | tf_op jit(solution)/shard_map/ppermute | solution.py:49
  (2 other events, 1.3 us)
where the time goes:
time: 362 us; the launch traced here: 359 us
  blocking collectives  140 us (39%)
  starting transfers between devices  86.4 us (24%)
  other arithmetic  78.1 us (22%)
  local copies, waits for them, and re-layouts  33.3 us (9%)
  between operations  14 us (4%)
  waiting for transfers between devices  7.57 us (2%)
    psum x16, blocking collectives, one_axis_at_a_time(): return functools.reduce(lax.psum, axes, shard)  140 us
    ppermute x10, starting transfers between devices, padded_2(): lax.ppermute(last, axis, up)  39.3 us
    scatter-add x1, other arithmetic, per_device(): coarse_count = jnp.zeros(block_rows * block_cols, jnp.float32).at[held_fl...  13.3 us
    ppermute x4, starting transfers between devices, extended(): lax.ppermute(lax.slice_in_dim(block, 0, width, axis=dim), axis, backward)  13.3 us
    scatter-add x1, other arithmetic, per_device(): sources = jnp.zeros(block_rows * block_cols, jnp.float32).at[held_flat].a...  13.1 us
    ppermute x10, starting transfers between devices, padded_2(): lax.ppermute(leading, axis, [(b, a) for a, b in up])  12.9 us
    gather x1, local copies, waits for them, and re-layouts, per_device(): volt.reshape(-1)[held_flat]  11.8 us
    gather x1, local copies, waits for them, and re-layouts, per_device(): at_fine = weight * solution.reshape(-1)[fine_index]  11.8 us
  transfers between devices with their start and end apart: 31, of which 3 were waited for; matrix products, arithmetic and copies ran while one was open for 30% of the time, Pallas kernels for 0%

commit v1 on v0

v1 whole, which is shorter than its diff:
```python
import functools

import jax
import jax.numpy as jnp
from jax import lax
from jax.experimental import pallas as pl
from jax.experimental.pallas import tpu as pltpu
from jax.sharding import PartitionSpec as P

MESH = pl.DeviceIdType.MESH
F32, BF16, I32 = jnp.float32, jnp.bfloat16, jnp.int32
GROUP = 16
NB = 4
OWN = 16
TILE = 512
ROWS = TILE + 2 * OWN
COARSE = 128
VIA = 2.0
CG = 4.0
RELAX = 0.8
NN = (((1,), (0,)), ((), ()))
NT = (((1,), (1,)), ((), ()))


def iota(shape, dim):
    return lax.broadcasted_iota(I32, shape, dim)


def dot(a, b, dims):
    return lax.dot_general(a, b, dims, preferred_element_type=F32)


def parts(x, n):
    out = []
    for _ in range(n):
        p = x.astype(BF16)
        out.append(p)
        x = x - p.astype(F32)
    return out


def kernel(
    nrow, ncol,
    amp_h, mask_h, leak_h, cleak, cinit, vfine, vcoarse, vcount,
    fine_h, coarse_o,
    amp, mask, leak, rt, ct, cva, cvb, field, dinv, diag, inj,
    req, held, look, atvia, vals, arrived,
    crow, ccol, tbig, htop, hbot, hleft, hright, hcorner, csend,
    mom, red_a, red_b, outb, ubuf, seam, crecv, srecv,
    in_sem, out_sem, rq_s, rq_r, rs_s, rs_r, ar_s, ar_r,
    ha_s, ha_r, ra_s, ra_r, rb_s, rb_r, ce_s, ce_r,
):
    slots = ncol * 128
    ri, ci = lax.axis_index("row"), lax.axis_index("col")

    loads = []
    for n, (src, dst) in enumerate(((leak_h, leak), (amp_h, amp), (mask_h, mask))):
        for j in range(NB):
            cp = pltpu.make_async_copy(src.at[:, pl.ds(j * 128, 128)], dst.at[j], in_sem.at[n, j])
            cp.start()
            loads.append(cp)

    for buf in (htop, hbot, hleft, hright, hcorner, crecv):
        buf[...] = jnp.zeros(buf.shape, F32)

    bar = pltpu.get_barrier_semaphore()
    for d in range(1, ncol):
        pl.semaphore_signal(bar, inc=1, device_id={"col": lax.rem(ci + d, ncol)}, device_id_type=MESH)
    for d in range(1, nrow):
        pl.semaphore_signal(bar, inc=1, device_id={"row": lax.rem(ri + d, nrow)}, device_id_type=MESH)
    for dr in (1, nrow - 1):
        for dc in (1, ncol - 1):
            pl.semaphore_signal(
                bar, inc=1,
                device_id={"row": lax.rem(ri + dr, nrow), "col": lax.rem(ci + dc, ncol)},
                device_id_type=MESH,
            )
    pl.semaphore_wait(bar, ncol + nrow + 2)

    lane = iota((1, 128), 1)

    def exchange(src, dst, ssem, rsem):
        cps = []
        for d in range(1, ncol):
            cp = pltpu.make_async_remote_copy(
                src_ref=src.at[d], dst_ref=dst.at[ci], send_sem=ssem.at[d], recv_sem=rsem.at[d],
                device_id={"col": lax.rem(ci + d, ncol)}, device_id_type=MESH,
            )
            cp.start()
            cps.append(cp)
        return cps

    def make_req(d, _):
        o = lax.rem(ci + d, ncol)
        idx = vcoarse[:, pl.ds(pl.multiple_of(o * 128, 128), 128)]
        node = lax.shift_right_logical(idx, lax.full_like(idx, (slots).bit_length() - 1)) * 128 + (idx & 127)
        r = jnp.where(lane < vcount[0, o], node, -1)
        req[d] = r
        return _

    lax.fori_loop(0, ncol, make_req, 0)
    held[ci] = req[0]
    rq = exchange(req, held, rq_s, rq_r)

    def make_fine(o, _):
        at = pl.ds(pl.multiple_of(o * 128, 128), 128)
        idx = vfine[:, at]
        live = lane < vcount[0, o]
        r = jnp.where(live, idx >> 9, -1)
        c = idx & 511
        for q in range(4):
            i = iota((128, 128), 0) + q * 128
            rt[q * 128:(q + 1) * 128, at] = jnp.where(i == r, 1.0, 0.0).astype(BF16)
            ct[q * 128:(q + 1) * 128, at] = jnp.where(i == c, 1.0, 0.0).astype(BF16)
        return _

    lax.fori_loop(0, ncol, make_fine, 0)
    for cp in loads[:NB]:
        cp.wait()
    for h in range(2):
        t = dot(rt[...], ct[h * 256:(h + 1) * 256, :], NT)
        for q in range(2):
            j = 2 * h + q
            dg = 4.0 + leak[j] + VIA * t[:, q * 128:(q + 1) * 128]
            diag[j] = dg
            dinv[j, OWN:OWN + TILE] = 1.0 / dg

    row8 = iota((8, 128), 1)

    def halo_copies(f, src):
        up, dn = lax.rem(ri + nrow - 1, nrow), lax.rem(ri + 1, nrow)
        lf, rg = lax.rem(ci + ncol - 1, ncol), lax.rem(ci + 1, ncol)
        hu, hd, hl, hr = ri > 0, ri < nrow - 1, ci > 0, ci < ncol - 1
        first, last = pl.ds(OWN, 8), pl.ds(OWN + TILE - 8, 8)
        own = pl.ds(0, NB)
        plan = (
            (hu, hd, src.at[own, first], hbot.at[f], {"row": up}),
            (hd, hu, src.at[own, last], htop.at[f], {"row": dn}),
            (hl, hr, csend.at[f, 0], hright.at[f], {"col": lf}),
            (hr, hl, csend.at[f, 1], hleft.at[f], {"col": rg}),
            (hu & hl, hd & hr, src.at[0, first], hcorner.at[f, 0], {"row": up, "col": lf}),
            (hu & hr, hd & hl, src.at[NB - 1, first], hcorner.at[f, 1], {"row": up, "col": rg}),
            (hd & hl, hu & hr, src.at[0, last], hcorner.at[f, 2], {"row": dn, "col": lf}),
            (hd & hr, hu & hl, src.at[NB - 1, last], hcorner.at[f, 3], {"row": dn, "col": rg}),
        )
        out = []
        for n, (to, frm, s, d, dev) in enumerate(plan):
            cp = pltpu.make_async_remote_copy(
                src_ref=s, dst_ref=d, send_sem=ha_s.at[f, n], recv_sem=ha_r.at[f, n],
                device_id=dev, device_id_type=MESH,
            )
            out.append((to, frm, cp))
        return out

    def halo_start(f, src):
        own = slice(OWN, OWN + TILE)
        csend[f, 0] = jnp.transpose(src[0, own])[:8]
        csend[f, 1] = jnp.transpose(src[NB - 1, own])[120:]
        cps = halo_copies(f, src)
        for to, _, cp in cps:
            pl.when(to)(cp.start)
        return cps

    def halo_finish(f, dst, cps):
        for _, frm, cp in cps:
            pl.when(frm)(cp.wait_recv)
        dst[0:NB, OWN - 8:OWN] = htop[f]
        dst[0:NB, OWN + TILE:OWN + TILE + 8] = hbot[f]
        x = jnp.concatenate([hright[f], jnp.zeros((112, TILE), F32), hleft[f]], axis=0)
        dst[NB, OWN:OWN + TILE] = jnp.transpose(x)
        near = row8 < 64
        dst[NB, OWN + TILE:OWN + TILE + 8] = jnp.where(near, hcorner[f, 0], hcorner[f, 1])
        dst[NB, OWN - 8:OWN] = jnp.where(near, hcorner[f, 2], hcorner[f, 3])

    def halo_sent(cps):
        for to, _, cp in cps:
            pl.when(to)(cp.wait_send)

    for buf in (dinv, field.at[0], field.at[1], field.at[2], field.at[3]):
        buf[:, 0:8] = jnp.zeros((NB + 1, 8, 128), F32)
        buf[:, ROWS - 8:ROWS] = jnp.zeros((NB + 1, 8, 128), F32)
    dcp = halo_start(0, dinv)

    u = cinit[...]
    uparts = parts(u, 3)
    ci128 = iota((128, 128), 0)
    for d in range(ncol):
        k = lax.rem(ci + ncol - d, ncol)
        if d:
            rq[d - 1].wait_recv()
        at = pl.ds(pl.multiple_of(k * 128, 128), 128)
        idx = held[k]
        crow[:, at] = jnp.where(ci128 == (idx >> 7), 1.0, 0.0).astype(BF16)
        ccol[:, at] = jnp.where(ci128 == (idx & 127), 1.0, 0.0).astype(BF16)
    t = dot(uparts[0], ccol[...], NN)
    for p in uparts[1:]:
        t = t + dot(p, ccol[...], NN)
    tbig[...] = t
    for d in range(ncol):
        k = lax.rem(ci + d, ncol)
        at = pl.ds(pl.multiple_of(k * 128, 128), 128)
        idx = held[k]
        look[d] = jnp.sum(jnp.where(ci128 == (idx >> 7), tbig[:, at], 0.0), axis=0, keepdims=True)
    atvia[ci] = look[0]
    rs = exchange(look, atvia, rs_s, rs_r)

    cdiag = 4.0 * CG + cleak[...] + VIA * dot(crow[...], ccol[...], NT)
    rdiag = RELAX / cdiag

    def coarse_start(s, u):
        ubuf[s] = u
        seam_t = jnp.transpose(u)
        tbig[:, 0:128] = seam_t
        for e, j in enumerate((0, GROUP - 1)):
            seam[s, e] = jnp.concatenate(
                [seam_t[g * GROUP + j:g * GROUP + j + 1] for g in range(128 // GROUP)], axis=0
            )
        up, dn = lax.rem(ri + nrow - 1, nrow), lax.rem(ri + 1, nrow)
        lf, rg = lax.rem(ci + ncol - 1, ncol), lax.rem(ci + 1, ncol)
        true = ri >= 0
        plan = (
            (ri > 0, ri < nrow - 1, ubuf.at[s, pl.ds(0, 8)], crecv.at[s, 1], {"row": up}),
            (ri < nrow - 1, ri > 0, ubuf.at[s, pl.ds(120, 8)], crecv.at[s, 0], {"row": dn}),
            (None, None, seam.at[s, 0], srecv.at[s, 1], {"col": lf}),
            (None, None, seam.at[s, 1], srecv.at[s, 0], {"col": rg}),
        )
        cps = []
        for n, (to, frm, sr, ds, dev) in enumerate(plan):
            cp = pltpu.make_async_remote_copy(
                src_ref=sr, dst_ref=ds, send_sem=ce_s.at[s, n], recv_sem=ce_r.at[s, n],
                device_id=dev, device_id_type=MESH,
            )
            if to is None:
                cp.start()
            else:
                pl.when(to)(cp.start)
            cps.append((to, frm, cp))
        return cps

    def coarse_beside(s, u, cps):
        for _, frm, cp in cps:
            if frm is None:
                cp.wait_recv()
            else:
                pl.when(frm)(cp.wait_recv)
        li, si = iota((128, 128), 1), ci128
        up = jnp.where(si == 0, crecv[s, 0, 7:8, :], pltpu.roll(u, 1, 0))
        dn = jnp.where(si == 127, crecv[s, 1, 0:1, :], pltpu.roll(u, 127, 0))
        g = iota((8, 128), 0)
        fl, fr = srecv[s, 0], srecv[s, 1]
        fl = jnp.where(ci == 0, jnp.where(g == 0, 0.0, pltpu.roll(fl, 1, 0)), fl)
        fr = jnp.where(ci == ncol - 1, jnp.where(g == 7, 0.0, pltpu.roll(fr, 7, 0)), fr)

        def spread(x):
            return jnp.concatenate([jnp.broadcast_to(x[q:q + 1], (GROUP, 128)) for q in range(8)], axis=0)

        x = jnp.transpose(jnp.where(si % GROUP == 0, spread(fl), spread(fr)))
        left = jnp.where(li % GROUP == 0, x, pltpu.roll(u, 1, 1))
        right = jnp.where(li % GROUP == GROUP - 1, x, pltpu.roll(u, 127, 1))
        return up + dn + left + right

    def coarse_sent(cps):
        for to, _, cp in cps:
            if to is None:
                cp.wait_send()
            else:
                pl.when(to)(cp.wait_send)

    c0 = coarse_start(0, u)
    for cp in loads[NB:]:
        cp.wait()
    halo_finish(0, dinv, dcp)

    def make_inj(o):
        at = pl.ds(pl.multiple_of(o * 128, 128), 128)
        p = parts(atvia[o], 2)
        col = ct[:, at]
        cva[:, at] = col * p[0]
        cvb[:, at] = col * p[1]

    for d in range(ncol):
        if d:
            rs[d - 1].wait_recv()
        make_inj(lax.rem(ci + ncol - d, ncol))
    v0 = field.at[0]
    for h in range(2):
        hs = slice(h * 256, (h + 1) * 256)
        t = dot(rt[...], cva[hs, :], NT) + dot(rt[...], cvb[hs, :], NT)
        for q in range(2):
            j = 2 * h + q
            rhs = amp[j] * mask[j].astype(F32) + VIA * t[:, q * 128:(q + 1) * 128]
            v0[j, OWN:OWN + TILE] = rhs * dinv[j, OWN:OWN + TILE]
    fcp = halo_start(1, v0)
    halo_finish(1, v0, fcp)

    first_lane, last_lane = row8 == 0, row8 == 127

    def beside(v, r):
        c = [v[j, pl.ds(r, 8)] for j in range(NB + 1)]
        rr = [pltpu.roll(x, 1, 1) for x in c]
        rl = [pltpu.roll(x, 127, 1) for x in c]
        out = []
        for j in range(NB + 1):
            left = jnp.where(first_lane, rr[(j - 1) % (NB + 1)], rr[j])
            right = jnp.where(last_lane, rl[(j + 1) % (NB + 1)], rl[j])
            out.append(v[j, pl.ds(r - 1, 8)] + v[j, pl.ds(r + 1, 8)] + left + right)
        return c, out

    def power(k):
        v, nxt = field.at[k], field.at[k + 1] if k < 3 else None
        count = (4, 4, 2, 1)[k]

        def rows(r, sums):
            c, nb = beside(v, r)
            sums = list(sums) if sums is not None else None
            for j in range(NB + 1):
                w = None
                if nxt is not None:
                    w = dinv[j, pl.ds(r, 8)] * nb[j]
                    nxt[j, pl.ds(r, 8)] = w
                if sums is not None and j < NB:
                    dv = diag[j, pl.ds(r - OWN, 8)] * c[j]
                    av = dv - nb[j]
                    sums[0] += c[j] * av
                    if count > 1:
                        sums[1] += w * av
                    if count > 2:
                        sums[2] += c[j] * dv
                        sums[3] += c[j] * nb[j]
            return tuple(sums) if sums is not None else None

        if nxt is not None:
            rows(OWN - 8, None)
            rows(OWN + TILE, None)

        def step(i, sums):
            return rows(pl.multiple_of(OWN + i * 8, 8), sums)

        z = jnp.zeros((8, 128), F32)
        return lax.fori_loop(0, TILE // 8, step, (z,) * count, unroll=2)

    n = 0
    for k in range(4):
        for s in power(k):
            mom[n // 8, n % 8:n % 8 + 1] = jnp.sum(s, axis=0, keepdims=True)
            n += 1
    mom[1, 3:8] = jnp.zeros((5, 128), F32)

    def reduce(src, buf, axis, me, size, ssem, rsem):
        cps = []
        for d in range(1, size):
            cp = pltpu.make_async_remote_copy(
                src_ref=src, dst_ref=buf.at[me], send_sem=ssem.at[d], recv_sem=rsem.at[d],
                device_id={axis: lax.rem(me + d, size)}, device_id_type=MESH,
            )
            cp.start()
            cps.append(cp)
        buf[me] = src[...]
        for cp in cps:
            cp.wait_recv()
        t = buf[0]
        for q in range(1, size):
            t = t + buf[q]
        for cp in cps:
            cp.wait_send()
        return t

    mom[...] = reduce(mom, red_a, "col", ci, ncol, ra_s, ra_r)
    tot = reduce(mom, red_b, "row", ri, nrow, rb_s, rb_r)
    tot = jnp.sum(tot, axis=2, keepdims=True)

    def m(q):
        return jnp.broadcast_to(tot[q // 8, q % 8:q % 8 + 1], (1, 128))

    eta = [m(q) for q in (0, 1, 4, 5, 8, 9, 10)]
    nu = [m(q) for q in (2, 3, 6, 7)]
    hm = [[eta[i + j] for j in range(4)] for i in range(4)]
    low = [[None] * 4 for _ in range(4)]
    piv = []
    for j in range(4):
        pj = hm[j][j]
        for q in range(j):
            pj = pj - low[j][q] * low[j][q] * piv[q]
        ok = pj > 1e-6 * hm[j][j]
        piv.append(pj)
        inv = jnp.where(ok, 1.0 / jnp.where(ok, pj, 1.0), 0.0)
        low[j][j] = inv
        for i in range(j + 1, 4):
            e = hm[i][j]
            for q in range(j):
                e = e - low[i][q] * low[j][q] * piv[q]
            low[i][j] = e * inv
    y = list(nu)
    for i in range(4):
        for q in range(i):
            y[i] = y[i] - low[i][q] * y[q]
    y = [y[i] * low[i][i] for i in range(4)]
    for i in (2, 1, 0):
        for q in range(i + 1, 4):
            y[i] = y[i] - low[q][i] * y[q]
    coef = [jnp.broadcast_to(c, (8, 128)) for c in y]

    def combine(i, _):
        r = pl.multiple_of(i * 16, 16)
        for j in range(NB):
            at = slice(j * 128, (j + 1) * 128)
            acc = []
            for q in range(2):
                rq_ = pl.ds(OWN + r + 8 * q, 8)
                a = coef[0] * field[0, j, rq_]
                for k in range(1, 4):
                    a = a + coef[k] * field[k, j, rq_]
                acc.append(a)
            a = jnp.concatenate(acc, axis=0)
            outb[pl.ds(r, 16), at] = a
            pa, pb = parts(a, 2)
            cva[pl.ds(r, 16), at] = pa
            cvb[pl.ds(r, 16), at] = pb
        return _

    lax.fori_loop(0, TILE // 16, combine, 0)
    ocp = pltpu.make_async_copy(outb, fine_h, out_sem)
    ocp.start()

    for o in range(0, ncol, 2):
        at = slice(o * 128, (o + 2) * 128)
        t = dot(cva[:, 0:TILE], ct[:, at], NN) + dot(cvb[:, 0:TILE], ct[:, at], NN)
        s = VIA * jnp.sum(t * rt[:, at].astype(F32), axis=0, keepdims=True)
        vals[o] = s[:, 0:128]
        vals[o + 1] = s[:, 128:256]
    arrived[ci] = vals[ci]
    ar = []
    for d in range(1, ncol):
        o = lax.rem(ci + d, ncol)
        cp = pltpu.make_async_remote_copy(
            src_ref=vals.at[o], dst_ref=arrived.at[ci], send_sem=ar_s.at[d], recv_sem=ar_r.at[d],
            device_id={"col": o}, device_id_type=MESH,
        )
        cp.start()
        ar.append(cp)

    p0 = u + rdiag * (CG * coarse_beside(0, u, c0) - cdiag * u)

    src = jnp.zeros((128, 128), F32)
    for d in range(ncol):
        if d:
            ar[d - 1].wait_recv()
        k = lax.rem(ci + ncol - d, ncol)
        at = pl.ds(pl.multiple_of(k * 128, 128), 128)
        pp = parts(arrived[k], 3)
        col = ccol[:, at]
        for n in range(3):
            rt[n * 128:(n + 1) * 128, at] = col * pp[n]
    for n in range(3):
        src = src + dot(crow[...], rt[n * 128:(n + 1) * 128, :], NT)
    u1 = p0 + rdiag * src
    c1 = coarse_start(1, u1)
    coarse_o[...] = u1 + rdiag * (src + CG * coarse_beside(1, u1, c1) - cdiag * u1)

    for cp in rq + rs + ar:
        cp.wait_send()
    halo_sent(dcp)
    halo_sent(fcp)
    coarse_sent(c0)
    coarse_sent(c1)
    ocp.wait()


def solution(mesh):
    nrow, ncol = mesh.shape["row"], mesh.shape["col"]
    slots = ncol * 128
    dma = pltpu.SemaphoreType.DMA

    def step(*args):
        vm = pl.BlockSpec(memory_space=pltpu.VMEM)
        anyspace = pl.BlockSpec(memory_space=pl.ANY)
        slab = (NB, TILE, 128)
        row = (ncol, 1, 128)
        return pl.pallas_call(
            functools.partial(kernel, nrow, ncol),
            out_shape=(
                jax.ShapeDtypeStruct((TILE, TILE), F32),
                jax.ShapeDtypeStruct((COARSE, COARSE), F32),
            ),
            in_specs=[anyspace, anyspace, anyspace, vm, vm, vm, vm, pl.BlockSpec(memory_space=pltpu.SMEM)],
            out_specs=(anyspace, vm),
            scratch_shapes=[
                pltpu.VMEM(slab, F32), pltpu.VMEM(slab, I32), pltpu.VMEM(slab, F32),
                pltpu.VMEM((TILE, slots), BF16), pltpu.VMEM((TILE, slots), BF16),
                pltpu.VMEM((TILE, slots), BF16), pltpu.VMEM((TILE, slots), BF16),
                pltpu.VMEM((4, NB + 1, ROWS, 128), F32), pltpu.VMEM((NB + 1, ROWS, 128), F32),
                pltpu.VMEM(slab, F32), pltpu.VMEM((8, 128), F32),
                pltpu.VMEM(row, I32), pltpu.VMEM(row, I32), pltpu.VMEM(row, F32), pltpu.VMEM(row, F32),
                pltpu.VMEM(row, F32), pltpu.VMEM(row, F32),
                pltpu.VMEM((128, slots), BF16), pltpu.VMEM((128, slots), BF16), pltpu.VMEM((128, slots), F32),
                pltpu.VMEM((2, NB, 8, 128), F32), pltpu.VMEM((2, NB, 8, 128), F32),
                pltpu.VMEM((2, 8, TILE), F32), pltpu.VMEM((2, 8, TILE), F32),
                pltpu.VMEM((2, 4, 8, 128), F32), pltpu.VMEM((2, 2, 8, TILE), F32),
                pltpu.VMEM((2, 8, 128), F32), pltpu.VMEM((ncol, 2, 8, 128), F32), pltpu.VMEM((nrow, 2, 8, 128), F32),
                pltpu.VMEM((TILE, TILE), F32),
                pltpu.VMEM((2, 128, 128), F32), pltpu.VMEM((2, 2, 8, 128), F32),
                pltpu.VMEM((2, 2, 8, 128), F32), pltpu.VMEM((2, 2, 8, 128), F32),
                dma((3, NB)), dma(()),
                dma((ncol,)), dma((ncol,)), dma((ncol,)), dma((ncol,)), dma((ncol,)), dma((ncol,)),
                dma((2, 8)), dma((2, 8)), dma((ncol,)), dma((ncol,)), dma((nrow,)), dma((nrow,)),
                dma((2, 4)), dma((2, 4)),
            ],
            compiler_params=pltpu.CompilerParams(collective_id=0, has_side_effects=True, vmem_limit_bytes=50 << 20),
        )(*args)

    spec = P("row", "col")
    return jax.shard_map(
        step, mesh=mesh, in_specs=(spec,) * 8, out_specs=(spec, spec), check_vma=False
    )
```

time: 362 us -> 71.4 us (0.20)
  blocking collectives: 140 us -> 0 us
  starting transfers between devices: 86.4 us -> 0 us
  other arithmetic: 78.1 us -> 0 us
  Pallas kernels: 0 us -> 62.6 us
  local copies, waits for them, and re-layouts: 33.3 us -> 7.77 us
  between operations: 14 us -> 0.66 us
  waiting for transfers between devices: 7.57 us -> 0 us
    psum x16 -> x0, blocking collectives: 140 us -> none  [one_axis_at_a_time(): return functools.reduce(lax.psum, axes, shard)]
    ppermute x28 -> x0, starting transfers between devices: 70.5 us -> none  [the longest x10 39.3 us: padded_2(): lax.ppermute(last, axis, up)]
    pallas_call x0 -> x1, Pallas kernels: none -> 62.6 us  [step(): pl.pallas_call(functools.partial(kernel, nrow, ncol), out_shape=(jax.Shap...]
    scatter-add x4 -> x0, other arithmetic: 49.4 us -> none  [the longest x1 13.3 us: per_device(): coarse_count = jnp.zeros(block_rows * block_cols, jnp.float32).at[held_fl...]
    gather x2 -> x0, local copies, waits for them, and re-layouts: 23.6 us -> none  [the longest x1 11.8 us: per_device(): volt.reshape(-1)[held_flat]]
    all_to_all x3 -> x0, starting transfers between devices: 15.9 us -> none  [the longest x1 8.98 us: per_device(): held = lax.all_to_all(request, COL, split_axis=0, concat_axis=0, tiled=True)]
    reduce_sum x4 -> x0, other arithmetic: 10.8 us -> none  [paired_sum(): jnp.sum(second)]
    div x4 -> x0, other arithmetic: 10.2 us -> none  [per_device(): precond = residual / fine_diag]
  transfers between devices with their start and end apart: 31 -> 0, of which waited for: 3 -> 0; matrix products, arithmetic and copies ran while one was open for 30% -> 0% of each run, Pallas kernels for 0% -> 0%
where the time goes in v1:
time: 71.4 us; the launch traced here: 71 us
  Pallas kernels  62.6 us (88%)
  local copies, waits for them, and re-layouts  7.77 us (11%)
    pallas_call x1, Pallas kernels, step(): pl.pallas_call(functools.partial(kernel, nrow, ncol), out_shape=(jax.Shap...  62.6 us
    unnamed x16, local copies, waits for them, and re-layouts  7.77 us

profile of v1, /device:TPU:0, one launch (start us, length us, event | category | flops | bytes accessed | tf_op | source)
XLA Modules:
  0.0 71.0 jit_solution(18041560587343950345)
XLA Ops:
  0.6 0.0 copy-start
  0.6 1.2 %copy-done = f32[512,512]{1,0:T(8,128)S(1)} copy-done((f32[512,512]{1,0:T(8,128)S(1)}, f32[512,512]{1,0:T(8,128)}, u32[]{:S(2)}) %copy-start) | copy-done | bytes 1048600
  1.9 0.0 copy-start.1
  1.9 1.2 %copy-done.1 = s32[512,512]{1,0:T(8,128)S(1)} copy-done((s32[512,512]{1,0:T(8,128)S(1)}, s32[512,512]{1,0:T(8,128)}, u32[]{:S(2)}) %copy-start.1) | copy-done | bytes 1048600
  3.1 0.0 copy-start.2
  3.1 0.8 %copy-done.2 = f32[128,128]{1,0:T(8,128)S(1)} copy-done((f32[128,128]{1,0:T(8,128)S(1)}, f32[128,128]{1,0:T(8,128)}, u32[]{:S(2)}) %copy-start.2) | copy-done | bytes 65560
  3.9 0.0 copy-start.3
  3.9 0.8 %copy-done.3 = f32[128,128]{1,0:T(8,128)S(1)} copy-done((f32[128,128]{1,0:T(8,128)S(1)}, f32[128,128]{1,0:T(8,128)}, u32[]{:S(2)}) %copy-start.3) | copy-done | bytes 65560
  4.8 0.0 copy-start.4
  4.8 0.7 copy-done.4
  5.5 0.0 copy-start.5
  5.5 0.7 copy-done.5
  6.2 0.0 copy-start.6
  6.2 0.7 copy-done.6
  6.8 62.6 %shard_map.95 = (f32[512,512]{1,0:T(8,128)S(1)}, f32[128,128]{1,0:T(8,128)S(1)}) custom-call(f32[512,512]{1,0:T(8,128)S(1)} %copy-done, s32[512,512]{1,0:T(8,128)S(1)} %copy-done.1, f32[512,512]{1,0:T(8,128)} %leak_h.1, f32[128,128]{1,0:T(8,128)S(1)} %copy-done.2, f32[128,128]{1,0:T(8,128)S(1)} %copy-done.3, s32[1,2048]{1,0:T(1,128)S(1)} %copy-done.4, ...), custom_call_target="tpu_custom_call" | custom-call | tf_op jit(solution)/shard_map/pallas_call | solution.py:479
  69.4 1.0 %copy.12 = f32[512,512]{1,0:T(8,128)} copy(f32[512,512]{1,0:T(8,128)S(1)} %get-tuple-element.4) | data formatting | bytes 2097152
  70.4 0.6 copy.13
Async XLA Ops:
  0.6 1.2 %copy-start = (f32[512,512]{1,0:T(8,128)S(1)}, f32[512,512]{1,0:T(8,128)}, u32[]{:S(2)}) copy-start(f32[512,512]{1,0:T(8,128)} %amp_h.1) | copy-start | bytes 3145732
  1.9 1.2 %copy-start.1 = (s32[512,512]{1,0:T(8,128)S(1)}, s32[512,512]{1,0:T(8,128)}, u32[]{:S(2)}) copy-start(s32[512,512]{1,0:T(8,128)} %mask_h.1) | copy-start | bytes 3145732
  3.1 0.8 %copy-start.2 = (f32[128,128]{1,0:T(8,128)S(1)}, f32[128,128]{1,0:T(8,128)}, u32[]{:S(2)}) copy-start(f32[128,128]{1,0:T(8,128)} %cleak.1) | copy-start | bytes 196612
  3.9 0.8 %copy-start.3 = (f32[128,128]{1,0:T(8,128)S(1)}, f32[128,128]{1,0:T(8,128)}, u32[]{:S(2)}) copy-start(f32[128,128]{1,0:T(8,128)} %cinit.1) | copy-start | bytes 196612
  4.8 0.7 copy-start.4
  5.5 0.7 copy-start.5
  6.2 0.7 copy-start.6

commit v2 on v1

v2 whole, which is shorter than its diff:
```python
import functools

import jax
import jax.numpy as jnp
from jax import lax
from jax.experimental import pallas as pl
from jax.experimental.pallas import tpu as pltpu
from jax.sharding import PartitionSpec as P

MESH = pl.DeviceIdType.MESH
F32, BF16, I32 = jnp.float32, jnp.bfloat16, jnp.int32
GROUP = 16
NB = 4
OWN = 16
TILE = 512
ROWS = TILE + 2 * OWN
COARSE = 128
VIA = 2.0
CG = 4.0
RELAX = 0.8
NN = (((1,), (0,)), ((), ()))
NT = (((1,), (1,)), ((), ()))


def iota(shape, dim):
    return lax.broadcasted_iota(I32, shape, dim)


def dot(a, b, dims):
    return lax.dot_general(a, b, dims, preferred_element_type=F32)


def parts(x, n):
    out = []
    for _ in range(n):
        p = x.astype(BF16)
        out.append(p)
        x = x - p.astype(F32)
    return out


class Phases:
    def __init__(self):
        self.open = None

    def __call__(self, name):
        if self.open is not None:
            self.open.__exit__(None, None, None)
        self.open = None
        if name:
            self.open = jax.named_scope(name)
            self.open.__enter__()


def peer_order(n):
    if n != 16:
        return list(range(n))
    return sorted(range(n), key=lambda d: min(d // 4, 4 - d // 4) + min(d % 4, 4 - d % 4))


def kernel(
    nrow, ncol,
    amp_h, mask_h, leak_h, cleak_h, cinit_h, vfine_h, vcoarse_h, vcount_h,
    fine_o, coarse_o,
    amp, mask, leak, rt, ct, cva, cvb, field, dinv, diag, inj, pa, pb,
    req, held, look, atvia, vals, arrived,
    crow, ccol, htop, hbot, hleft, hright, hcorner, csend,
    mom, red_a, red_b, split, ubuf, seam, crecv, srecv,
    cleak, cinit, vfine, vcoarse, vcount,
    in_sem, small_sem, rq_s, rq_r, rs_s, rs_r, ar_s, ar_r,
    ha_s, ha_r, ra_s, ra_r, rb_s, rb_r, ce_s, ce_r,
):
    slots = ncol * 128
    phase = Phases()
    phase("start")
    ri, ci = lax.axis_index("row"), lax.axis_index("col")

    small = []
    for n, (src, dst) in enumerate((
        (vcount_h, vcount), (vcoarse_h, vcoarse), (vfine_h, vfine), (cinit_h, cinit), (cleak_h, cleak)
    )):
        cp = pltpu.make_async_copy(src, dst, small_sem.at[n])
        cp.start()
        small.append(cp)
    loads = []
    for n, (src, dst) in enumerate(((leak_h, leak), (amp_h, amp), (mask_h, mask))):
        for j in range(NB):
            cp = pltpu.make_async_copy(src.at[:, pl.ds(j * 128, 128)], dst.at[j], in_sem.at[n, j])
            cp.start()
            loads.append(cp)

    for buf in (htop, hbot, hleft, hright, hcorner, crecv):
        buf[...] = jnp.zeros(buf.shape, F32)

    phase("barrier")
    order = peer_order(ncol)

    def peer(p, sign):
        if ncol != 16:
            return lax.rem(ci + (order[p] if sign > 0 else ncol - order[p]), ncol)
        dy, dx = order[p] // 4, order[p] % 4
        y, x = ci // 4, lax.rem(ci, 4)
        if sign < 0:
            dy, dx = 4 - dy, 4 - dx
        return lax.rem(y + dy, 4) * 4 + lax.rem(x + dx, 4)

    bar = pltpu.get_barrier_semaphore()
    for d in range(1, ncol):
        pl.semaphore_signal(bar, inc=1, device_id={"col": lax.rem(ci + d, ncol)}, device_id_type=MESH)
    for d in range(1, nrow):
        pl.semaphore_signal(bar, inc=1, device_id={"row": lax.rem(ri + d, nrow)}, device_id_type=MESH)
    for dr in (1, nrow - 1):
        for dc in (1, ncol - 1):
            pl.semaphore_signal(
                bar, inc=1,
                device_id={"row": lax.rem(ri + dr, nrow), "col": lax.rem(ci + dc, ncol)},
                device_id_type=MESH,
            )
    phase("wait_small")
    for cp in small:
        cp.wait()
    lane = iota((1, 128), 1)

    def exchange(src, dst, ssem, rsem, sign):
        cps = []
        for p in reversed(range(1, ncol)):
            cp = pltpu.make_async_remote_copy(
                src_ref=src.at[p], dst_ref=dst.at[p], send_sem=ssem.at[p], recv_sem=rsem.at[p],
                device_id={"col": peer(p, sign)}, device_id_type=MESH,
            )
            cp.start()
            cps.append(cp)
        return cps[::-1]

    phase("fine_onehot")
    for p in range(ncol):
        o = peer(p, 1)
        idx = vfine[:, pl.ds(pl.multiple_of(o * 128, 128), 128)]
        at = slice(p * 128, (p + 1) * 128)
        r = jnp.where(lane < vcount[0, o], idx >> 9, -1)
        c = idx & 511
        for q in range(4):
            i = iota((128, 128), 0) + q * 128
            rt[q * 128:(q + 1) * 128, at] = jnp.where(i == r, 1.0, 0.0).astype(BF16)
            ct[q * 128:(q + 1) * 128, at] = jnp.where(i == c, 1.0, 0.0).astype(BF16)
    phase("count_dot")
    for cp in loads[:NB]:
        cp.wait()
    for h in range(2):
        t = dot(rt[...], ct[h * 256:(h + 1) * 256, :], NT)
        for q in range(2):
            j = 2 * h + q
            dg = 4.0 + leak[j] + VIA * t[:, q * 128:(q + 1) * 128]
            diag[j] = dg
            dinv[j, OWN:OWN + TILE] = 1.0 / dg

    phase("barrier_wait")
    pl.semaphore_wait(bar, ncol + nrow + 2)

    phase("requests")
    for p in reversed(range(ncol)):
        o = peer(p, 1)
        idx = vcoarse[:, pl.ds(pl.multiple_of(o * 128, 128), 128)]
        node = lax.shift_right_logical(idx, lax.full_like(idx, (slots).bit_length() - 1)) * 128 + (idx & 127)
        (req if p else held)[p] = jnp.where(lane < vcount[0, o], node, -1)
    rq = exchange(req, held, rq_s, rq_r, 1)

    row8 = iota((8, 128), 1)

    def halo_copies(f, src):
        up, dn = lax.rem(ri + nrow - 1, nrow), lax.rem(ri + 1, nrow)
        lf, rg = lax.rem(ci + ncol - 1, ncol), lax.rem(ci + 1, ncol)
        hu, hd, hl, hr = ri > 0, ri < nrow - 1, ci > 0, ci < ncol - 1
        first, last = pl.ds(OWN, 8), pl.ds(OWN + TILE - 8, 8)
        own = pl.ds(0, NB)
        plan = (
            (hu, hd, src.at[own, first], hbot.at[f], {"row": up}),
            (hd, hu, src.at[own, last], htop.at[f], {"row": dn}),
            (hl, hr, csend.at[f, 0], hright.at[f], {"col": lf}),
            (hr, hl, csend.at[f, 1], hleft.at[f], {"col": rg}),
            (hu & hl, hd & hr, src.at[0, first], hcorner.at[f, 0], {"row": up, "col": lf}),
            (hu & hr, hd & hl, src.at[NB - 1, first], hcorner.at[f, 1], {"row": up, "col": rg}),
            (hd & hl, hu & hr, src.at[0, last], hcorner.at[f, 2], {"row": dn, "col": lf}),
            (hd & hr, hu & hl, src.at[NB - 1, last], hcorner.at[f, 3], {"row": dn, "col": rg}),
        )
        out = []
        for n, (to, frm, s, d, dev) in enumerate(plan):
            cp = pltpu.make_async_remote_copy(
                src_ref=s, dst_ref=d, send_sem=ha_s.at[f, n], recv_sem=ha_r.at[f, n],
                device_id=dev, device_id_type=MESH,
            )
            out.append((to, frm, cp))
        return out

    def halo_start(f, src):
        own = slice(OWN, OWN + TILE)
        csend[f, 0] = jnp.transpose(src[0, own])[:8]
        csend[f, 1] = jnp.transpose(src[NB - 1, own])[120:]
        cps = halo_copies(f, src)
        for to, _, cp in cps:
            pl.when(to)(cp.start)
        return cps

    def halo_finish(f, dst, cps):
        for _, frm, cp in cps:
            pl.when(frm)(cp.wait_recv)
        dst[0:NB, OWN - 8:OWN] = htop[f]
        dst[0:NB, OWN + TILE:OWN + TILE + 8] = hbot[f]
        x = jnp.concatenate([hright[f], jnp.zeros((112, TILE), F32), hleft[f]], axis=0)
        dst[NB, OWN:OWN + TILE] = jnp.transpose(x)
        near = row8 < 64
        dst[NB, OWN + TILE:OWN + TILE + 8] = jnp.where(near, hcorner[f, 0], hcorner[f, 1])
        dst[NB, OWN - 8:OWN] = jnp.where(near, hcorner[f, 2], hcorner[f, 3])

    def halo_sent(cps):
        for to, _, cp in cps:
            pl.when(to)(cp.wait_send)

    phase("dinv_halo")
    for buf in (dinv, field.at[0], field.at[1], field.at[2], field.at[3]):
        buf[:, 0:8] = jnp.zeros((NB + 1, 8, 128), F32)
        buf[:, ROWS - 8:ROWS] = jnp.zeros((NB + 1, 8, 128), F32)
    dcp = halo_start(0, dinv)

    phase("wait_req")
    u = cinit[...]
    split[0:256] = jnp.concatenate(parts(u, 2), axis=0)
    ci128 = iota((128, 128), 0)
    for p in range(ncol):
        if p:
            rq[p - 1].wait_recv()
        at = slice(p * 128, (p + 1) * 128)
        idx = held[p]
        crow[:, at] = jnp.where(ci128 == (idx >> 7), 1.0, 0.0).astype(BF16)
        ccol[:, at] = jnp.where(ci128 == (idx & 127), 1.0, 0.0).astype(BF16)
    phase("lookup")
    rs = [None] * ncol
    for n in reversed(range(ncol // 2)):
        at = slice(n * 256, (n + 1) * 256)
        t = dot(split[0:256], ccol[:, at], NN)
        t = jnp.sum((t[:128] + t[128:]) * crow[:, at].astype(F32), axis=0, keepdims=True)
        for p in (2 * n + 1, 2 * n):
            (look if p else atvia)[p] = t[:, (p - 2 * n) * 128:(p - 2 * n + 1) * 128]
            if p:
                rs[p] = pltpu.make_async_remote_copy(
                    src_ref=look.at[p], dst_ref=atvia.at[p], send_sem=rs_s.at[p], recv_sem=rs_r.at[p],
                    device_id={"col": peer(p, -1)}, device_id_type=MESH,
                )
                rs[p].start()
    rs = rs[1:]

    phase("coarse_diag")
    cdiag = 4.0 * CG + cleak[...] + VIA * dot(crow[...], ccol[...], NT)
    rdiag = RELAX / cdiag

    def coarse_start(s, u):
        ubuf[s] = u
        seam_t = jnp.transpose(u)
        for e, j in enumerate((0, GROUP - 1)):
            seam[s, e] = jnp.concatenate(
                [seam_t[g * GROUP + j:g * GROUP + j + 1] for g in range(128 // GROUP)], axis=0
            )
        up, dn = lax.rem(ri + nrow - 1, nrow), lax.rem(ri + 1, nrow)
        lf, rg = lax.rem(ci + ncol - 1, ncol), lax.rem(ci + 1, ncol)
        true = ri >= 0
        plan = (
            (ri > 0, ri < nrow - 1, ubuf.at[s, pl.ds(0, 8)], crecv.at[s, 1], {"row": up}),
            (ri < nrow - 1, ri > 0, ubuf.at[s, pl.ds(120, 8)], crecv.at[s, 0], {"row": dn}),
            (None, None, seam.at[s, 0], srecv.at[s, 1], {"col": lf}),
            (None, None, seam.at[s, 1], srecv.at[s, 0], {"col": rg}),
        )
        cps = []
        for n, (to, frm, sr, ds, dev) in enumerate(plan):
            cp = pltpu.make_async_remote_copy(
                src_ref=sr, dst_ref=ds, send_sem=ce_s.at[s, n], recv_sem=ce_r.at[s, n],
                device_id=dev, device_id_type=MESH,
            )
            if to is None:
                cp.start()
            else:
                pl.when(to)(cp.start)
            cps.append((to, frm, cp))
        return cps

    def coarse_beside(s, u, cps):
        for _, frm, cp in cps:
            if frm is None:
                cp.wait_recv()
            else:
                pl.when(frm)(cp.wait_recv)
        li, si = iota((128, 128), 1), ci128
        up = jnp.where(si == 0, crecv[s, 0, 7:8, :], pltpu.roll(u, 1, 0))
        dn = jnp.where(si == 127, crecv[s, 1, 0:1, :], pltpu.roll(u, 127, 0))
        g = iota((8, 128), 0)
        fl, fr = srecv[s, 0], srecv[s, 1]
        fl = jnp.where(ci == 0, jnp.where(g == 0, 0.0, pltpu.roll(fl, 1, 0)), fl)
        fr = jnp.where(ci == ncol - 1, jnp.where(g == 7, 0.0, pltpu.roll(fr, 7, 0)), fr)

        def spread(x):
            return jnp.concatenate([jnp.broadcast_to(x[q:q + 1], (GROUP, 128)) for q in range(8)], axis=0)

        x = jnp.transpose(jnp.where(si % GROUP == 0, spread(fl), spread(fr)))
        left = jnp.where(li % GROUP == 0, x, pltpu.roll(u, 1, 1))
        right = jnp.where(li % GROUP == GROUP - 1, x, pltpu.roll(u, 127, 1))
        return up + dn + left + right

    def coarse_sent(cps):
        for to, _, cp in cps:
            if to is None:
                cp.wait_send()
            else:
                pl.when(to)(cp.wait_send)

    phase("coarse_start")
    c0 = coarse_start(0, u)
    for cp in loads[NB:]:
        cp.wait()
    phase("dinv_finish")
    halo_finish(0, dinv, dcp)

    def make_inj(o):
        at = pl.ds(pl.multiple_of(o * 128, 128), 128)
        p = parts(atvia[o], 2)
        col = ct[:, at]
        cva[:, at] = col * p[0]
        cvb[:, at] = col * p[1]

    v0 = field.at[0]
    half = ncol // 2
    for part in range(2):
        phase(f"wait_resp{part}")
        for p in range(part * half, (part + 1) * half):
            if p:
                rs[p - 1].wait_recv()
            at = slice(p * 128, (p + 1) * 128)
            pp = parts(atvia[p], 2)
            col = ct[:, at]
            cva[:, at] = col * pp[0]
            cvb[:, at] = col * pp[1]
        phase(f"inject_dot{part}")
        ks = slice(part * half * 128, (part + 1) * half * 128)
        for h in range(2):
            hs = slice(h * 256, (h + 1) * 256)
            t = dot(rt[:, ks], cva[hs, ks], NT) + dot(rt[:, ks], cvb[hs, ks], NT)
            for q in range(2):
                j = 2 * h + q
                tq = VIA * t[:, q * 128:(q + 1) * 128]
                if part == 0:
                    inj[j] = amp[j] * mask[j].astype(F32) + tq
                else:
                    z = (inj[j] + tq) * dinv[j, OWN:OWN + TILE]
                    v0[j, OWN:OWN + TILE] = z
                    za, zb = parts(z, 2)
                    pa[0, :, j * 128:(j + 1) * 128] = za
                    pb[0, :, j * 128:(j + 1) * 128] = zb
    phase("halo_start")
    fcp = halo_start(1, v0)

    def gather(k):
        for n in range(ncol // 2):
            at = slice(n * 256, (n + 1) * 256)
            t = dot(pa[k], ct[:, at], NN) + dot(pb[k], ct[:, at], NN)
            t = VIA * jnp.sum(t * rt[:, at].astype(F32), axis=0, keepdims=True)
            for p in (2 * n, 2 * n + 1):
                (vals if p else arrived)[p, k:k + 1] = t[:, (p - 2 * n) * 128:(p - 2 * n + 1) * 128]

    phase("gather0")
    gather(0)
    phase("halo_finish")
    halo_finish(1, v0, fcp)

    phase("powers")
    def beside(v, r, h):
        lanes = iota((h, 128), 1)
        first_lane, last_lane = lanes == 0, lanes == 127
        c = [v[j, pl.ds(r, h)] for j in range(NB + 1)]
        rr = [pltpu.roll(x, 1, 1) for x in c]
        rl = [pltpu.roll(x, 127, 1) for x in c]
        out = []
        for j in range(NB + 1):
            left = jnp.where(first_lane, rr[(j - 1) % (NB + 1)], rr[j])
            right = jnp.where(last_lane, rl[(j + 1) % (NB + 1)], rl[j])
            out.append(v[j, pl.ds(r - 1, h)] + v[j, pl.ds(r + 1, h)] + left + right)
        return c, out

    def power(k):
        v, nxt = field.at[k], field.at[k + 1] if k < 3 else None
        count = (4, 4, 2, 1)[k]

        def rows(r, h, sums):
            c, nb = beside(v, r, h)
            sums = list(sums) if sums is not None else None

            def add(n, x):
                for q in range(h // 8):
                    sums[n] = sums[n] + x[q * 8:(q + 1) * 8]

            for j in range(NB + 1):
                w = None
                if nxt is not None:
                    w = dinv[j, pl.ds(r, h)] * nb[j]
                    nxt[j, pl.ds(r, h)] = w
                if sums is not None and j < NB:
                    if nxt is not None:
                        wa, wb = parts(w, 2)
                        pa[k + 1, pl.ds(r - OWN, h), j * 128:(j + 1) * 128] = wa
                        pb[k + 1, pl.ds(r - OWN, h), j * 128:(j + 1) * 128] = wb
                    dv = diag[j, pl.ds(r - OWN, h)] * c[j]
                    av = dv - nb[j]
                    add(0, c[j] * av)
                    if count > 1:
                        add(1, w * av)
                    if count > 2:
                        add(2, c[j] * dv)
                        add(3, c[j] * nb[j])
            return tuple(sums) if sums is not None else None

        if nxt is not None:
            rows(OWN - 8, 8, None)
            rows(OWN + TILE, 8, None)

        def step(i, sums):
            return rows(pl.multiple_of(OWN + i * 16, 16), 16, sums)

        z = jnp.zeros((8, 128), F32)
        return lax.fori_loop(0, TILE // 16, step, (z,) * count, unroll=4)

    n = 0
    for k in range(4):
        for s in power(k):
            mom[n:n + 1] = jnp.sum(s, axis=0, keepdims=True)
            n += 1
    mom[11:16] = jnp.zeros((5, 128), F32)

    phase("lane_sum")
    t = jnp.sum(mom[...], axis=1, keepdims=True)
    red_a[ci] = jnp.sum(jnp.where(iota((16, 128), 0) == iota((16, 128), 1), t, 0.0), axis=0, keepdims=True)

    def reduce_start(buf, axis, me, size, ssem, rsem):
        cps = []
        for d in range(1, size):
            cp = pltpu.make_async_remote_copy(
                src_ref=buf.at[me], dst_ref=buf.at[me], send_sem=ssem.at[d], recv_sem=rsem.at[d],
                device_id={axis: lax.rem(me + d, size)}, device_id_type=MESH,
            )
            cp.start()
            cps.append(cp)
        return cps

    def reduce_finish(buf, size, cps):
        for cp in cps:
            cp.wait_recv()
        t = buf[0]
        for q in range(1, size):
            t = t + buf[q]
        return t

    ra = reduce_start(red_a, "col", ci, ncol, ra_s, ra_r)
    phase("gather1")
    gather(1)
    phase("reduce_col")
    red_b[ri] = reduce_finish(red_a, ncol, ra)
    rb = reduce_start(red_b, "row", ri, nrow, rb_s, rb_r)
    phase("gather23")
    gather(2)
    gather(3)
    ar = exchange(vals, arrived, ar_s, ar_r, 1)
    phase("sweep_pre")
    p0 = u + rdiag * (CG * coarse_beside(0, u, c0) - cdiag * u)
    phase("reduce_row")
    tot = reduce_finish(red_b, nrow, rb)

    phase("solve")
    def m(q):
        return jnp.broadcast_to(jnp.sum(jnp.where(lane == q, tot, 0.0), axis=1, keepdims=True), (1, 128))

    eta = [m(q) for q in (0, 1, 4, 5, 8, 9, 10)]
    nu = [m(q) for q in (2, 3, 6, 7)]
    hm = [[eta[i + j] for j in range(4)] for i in range(4)]
    low = [[None] * 4 for _ in range(4)]
    piv = []
    for j in range(4):
        pj = hm[j][j]
        for q in range(j):
            pj = pj - low[j][q] * low[j][q] * piv[q]
        ok = pj > 1e-6 * hm[j][j]
        piv.append(pj)
        inv = jnp.where(ok, 1.0 / jnp.where(ok, pj, 1.0), 0.0)
        low[j][j] = inv
        for i in range(j + 1, 4):
            e = hm[i][j]
            for q in range(j):
                e = e - low[i][q] * low[j][q] * piv[q]
            low[i][j] = e * inv
    y = list(nu)
    for i in range(4):
        for q in range(i):
            y[i] = y[i] - low[i][q] * y[q]
    y = [y[i] * low[i][i] for i in range(4)]
    for i in (2, 1, 0):
        for q in range(i + 1, 4):
            y[i] = y[i] - low[q][i] * y[q]
    phase("combine")

    def combine(i, _):
        r = pl.multiple_of(i * 16, 16)
        for j in range(NB):
            rows = pl.ds(OWN + r, 16)
            a = y[0] * field[0, j, rows]
            for k in range(1, 4):
                a = a + y[k] * field[k, j, rows]
            fine_o[pl.ds(r, 16), j * 128:(j + 1) * 128] = a
        return _

    lax.fori_loop(0, TILE // 16, combine, 0, unroll=4)

    phase("wait_vals")
    for p in range(ncol):
        if p:
            ar[p - 1].wait_recv()
        at = slice(p * 128, (p + 1) * 128)
        a = y[0] * arrived[p, 0:1]
        for k in range(1, 4):
            a = a + y[k] * arrived[p, k:k + 1]
        hot = crow[:, at]
        for n, x in enumerate(parts(a, 2)):
            cva[n * 128:(n + 1) * 128, at] = hot * x
    phase("sources")
    t = dot(cva[0:256, :], ccol[...], NT)
    src = t[:128] + t[128:]
    u1 = p0 + rdiag * src
    phase("edges1")
    c1 = coarse_start(1, u1)
    phase("sweep2")
    coarse_o[...] = u1 + rdiag * (src + CG * coarse_beside(1, u1, c1) - cdiag * u1)

    phase("drain")
    for cp in rq + rs + ar + ra + rb:
        cp.wait_send()
    halo_sent(dcp)
    halo_sent(fcp)
    coarse_sent(c0)
    coarse_sent(c1)
    phase("")


def solution(mesh):
    nrow, ncol = mesh.shape["row"], mesh.shape["col"]
    slots = ncol * 128
    dma = pltpu.SemaphoreType.DMA

    def step(*args):
        vm = pl.BlockSpec(memory_space=pltpu.VMEM)
        anyspace = pl.BlockSpec(memory_space=pl.ANY)
        hbm = pl.BlockSpec(memory_space=pltpu.HBM)
        slab = (NB, TILE, 128)
        row = (ncol, 1, 128)
        return pl.pallas_call(
            functools.partial(kernel, nrow, ncol),
            out_shape=(
                pltpu.VMEM((TILE, TILE), F32),
                pltpu.VMEM((COARSE, COARSE), F32),
            ),
            in_specs=[hbm] * 8,
            out_specs=(vm, vm),
            scratch_shapes=[
                pltpu.VMEM(slab, F32), pltpu.VMEM(slab, I32), pltpu.VMEM(slab, F32),
                pltpu.VMEM((TILE, slots), BF16), pltpu.VMEM((TILE, slots), BF16),
                pltpu.VMEM((TILE, slots), BF16), pltpu.VMEM((TILE, slots), BF16),
                pltpu.VMEM((4, NB + 1, ROWS, 128), F32), pltpu.VMEM((NB + 1, ROWS, 128), F32),
                pltpu.VMEM(slab, F32), pltpu.VMEM(slab, F32),
                pltpu.VMEM((4, TILE, TILE), BF16), pltpu.VMEM((4, TILE, TILE), BF16),
                pltpu.VMEM(row, I32), pltpu.VMEM(row, I32), pltpu.VMEM(row, F32), pltpu.VMEM(row, F32),
                pltpu.VMEM((ncol, 4, 128), F32), pltpu.VMEM((ncol, 4, 128), F32),
                pltpu.VMEM((128, slots), BF16), pltpu.VMEM((128, slots), BF16),
                pltpu.VMEM((2, NB, 8, 128), F32), pltpu.VMEM((2, NB, 8, 128), F32),
                pltpu.VMEM((2, 8, TILE), F32), pltpu.VMEM((2, 8, TILE), F32),
                pltpu.VMEM((2, 4, 8, 128), F32), pltpu.VMEM((2, 2, 8, TILE), F32),
                pltpu.VMEM((16, 128), F32), pltpu.VMEM((ncol, 1, 128), F32), pltpu.VMEM((nrow, 1, 128), F32),
                pltpu.VMEM((256, 128), BF16),
                pltpu.VMEM((2, 128, 128), F32), pltpu.VMEM((2, 2, 8, 128), F32),
                pltpu.VMEM((2, 2, 8, 128), F32), pltpu.VMEM((2, 2, 8, 128), F32),
                pltpu.VMEM((COARSE, COARSE), F32), pltpu.VMEM((COARSE, COARSE), F32),
                pltpu.VMEM((1, slots), I32), pltpu.VMEM((1, slots), I32), pltpu.SMEM((1, ncol), I32),
                dma((3, NB)), dma((5,)),
                dma((ncol,)), dma((ncol,)), dma((ncol,)), dma((ncol,)), dma((ncol,)), dma((ncol,)),
                dma((2, 8)), dma((2, 8)), dma((ncol,)), dma((ncol,)), dma((nrow,)), dma((nrow,)),
                dma((2, 4)), dma((2, 4)),
            ],
            compiler_params=pltpu.CompilerParams(collective_id=0, has_side_effects=True, vmem_limit_bytes=50 << 20),
        )(*[pltpu.with_memory_space_constraint(x, pltpu.HBM) for x in args])

    spec = P("row", "col")
    return jax.shard_map(
        step, mesh=mesh, in_specs=(spec,) * 8, out_specs=(spec, spec), check_vma=False
    )
```

time: 71.4 us -> 55 us (0.77)
  Pallas kernels: 62.6 us -> 52.7 us
  local copies, waits for them, and re-layouts: 7.77 us -> 1.6 us
    pallas_call x1, Pallas kernels: 62.6 us -> 52.7 us  [step(): pl.pallas_call(functools.partial(kernel, nrow, ncol), out_shape=(pltpu.VM...]
    unnamed x16 -> x2, local copies, waits for them, and re-layouts: 7.77 us -> 1.6 us
where the time goes in v2:
time: 55 us; the launch traced here: 54.9 us
  Pallas kernels  52.7 us (96%)
  local copies, waits for them, and re-layouts  1.6 us (3%)
  between operations  0.64 us (1%)
    pallas_call x1, Pallas kernels, step(): pl.pallas_call(functools.partial(kernel, nrow, ncol), out_shape=(pltpu.VM...  52.7 us
    unnamed x2, local copies, waits for them, and re-layouts  1.6 us

profile of v2, /device:TPU:0, one launch (start us, length us, event | category | flops | bytes accessed | tf_op | source)
XLA Modules:
  0.0 54.9 jit_solution(5501945564555733405)
XLA Ops:
  0.6 52.7 %shard_map.95 = (f32[512,512]{1,0:T(8,128)S(1)}, f32[128,128]{1,0:T(8,128)S(1)}) custom-call(f32[512,512]{1,0:T(8,128)} %amp_h.1, s32[512,512]{1,0:T(8,128)} %mask_h.1, f32[512,512]{1,0:T(8,128)} %leak_h.1, f32[128,128]{1,0:T(8,128)} %cleak_h.1, f32[128,128]{1,0:T(8,128)} %cinit_h.1, s32[1,2048]{1,0:T(1,128)} %vfine_h.1, s32[1,2048]{1,0:T(1,128)} %vcoarse_h.1, ...), custom_call_target="tpu_custom_call" | custom-call | tf_op jit(solution)/shard_map/pallas_call | solution.py:558
  53.3 1.0 %copy.12 = f32[512,512]{1,0:T(8,128)} copy(f32[512,512]{1,0:T(8,128)S(1)} %get-tuple-element.2) | data formatting | bytes 2097152
  54.3 0.6 %copy.13 = f32[128,128]{1,0:T(8,128)} copy(f32[128,128]{1,0:T(8,128)S(1)} %get-tuple-element.3) | data formatting | bytes 131072
